TPU v7x, 256 devices: a whole 4x4x8 slice. The times are simulated.
256 devices in a mesh: gx: 16 (over y, z_hi), gy: 16 (over z_lo, x, core).
Axes of the slice: x: 4, y: 4, z: 8 (z_hi: 4, z_lo: 2; z = z_hi * 2 + z_lo), core: 2. Of those that a mesh axis runs over, the one named last changes fastest.
Arguments:
- liquid_starting_warmth: float32 [64, 256, 1024], P('gx', 'gy'), may hold values from -6 to 6
- liquid_spreading_ratios: float32 [64, 256, 1024], P('gx', 'gy'), may hold values from 0.02 to 0.12
- liquid_advective_ratios: float32 [3, 64, 256, 1024], P(None, 'gx', 'gy'), may hold values from -0.08 to 0.08
- liquid_refresh_flags: int32 [64, 256, 8], P('gx', 'gy'), may hold values 0 or 1
- wall_starting_warmth: float32 [64, 256, 1024], P('gx', 'gy'), may hold values from -6 to 6
- wall_thermal_capacity: float32 [64, 256, 1024], P('gx', 'gy'), may hold values from 0.5 to 2
- thermal_conductance: float32 [64, 256, 1024], P('gx', 'gy'), may hold values from 0.5 to 15
- wall_energy_output: float32 [64, 256, 1024], P('gx', 'gy'), may hold values from -36 to 36
- coupling_partner_lookup: int32 [64, 256], P('gx', 'gy'), may hold values from 0 to 255, each once within a row
Outputs:
- fluid_after: float32 [64, 256, 1024], P('gx', 'gy')
- solid_after: float32 [64, 256, 1024], P('gx', 'gy')
Inputs may be any that keep to these rules, and one draw needn't show every extreme that they name: For each first index, the row of coupling_partner_lookup holds every number of 0 to 255 once.
All inputs are finite; a program needn't handle non-finite values. No bound on the sum of `liquid_refresh_flags` on one device may be relied on, other than what follows from the above.
Results may differ from a plain program's by a relative error of at most 0.00023.
Values sent between devices are 32-bit elements; how exact they have to be, the bound alone decides.
A program may use at most 64 MiB of HBM per device.

v0:
```python
import functools

import jax
import jax.numpy as jnp
from jax import lax
from jax.sharding import Mesh
from jax.sharding import PartitionSpec as P

SUBSTEPS = 4
ITERS = 4
ZB = 128
GY = ("gy_0", "gy_1", "gy_2")
GX_GY = ("gx_0", "gx_1", "gy_0", "gy_1", "gy_2")
GX = ("gx_0", "gx_1")


def laid_out(tiles, dim):
    shape = list(tiles.shape[1:])
    shape[dim] *= tiles.shape[0]
    return jnp.moveaxis(tiles, 0, dim).reshape(shape)


def sent_to_all(shard, axis):
    copies = jnp.broadcast_to(shard, (lax.axis_size(axis), *shard.shape))
    return lax.all_to_all(copies, axis, split_axis=0, concat_axis=0, tiled=True)


def gathered_copies(shard, axis, dim):
    return laid_out(sent_to_all(shard, axis), dim)


def with_halo(shard, sides, width):
    edges = {}
    for axis, dim in sides:
        devices, length = (lax.axis_size(axis), shard.shape[dim])
        up = [(i, (i + 1) % devices) for i in range(devices - 1)]
        last = lax.slice_in_dim(shard, length - width, length, axis=dim)
        initial = lax.slice_in_dim(shard, 0, width, axis=dim)
        edges[dim] = (
            lax.ppermute(last, axis, up),
            lax.ppermute(initial, axis, [(b, a) for a, b in up]),
        )
    done = []
    for _, dim in sides:
        low, high = edges[dim]
        around = [(width, width) if d in done else (0, 0) for d in range(shard.ndim)]
        shard = jnp.concatenate([jnp.pad(low, around), shard, jnp.pad(high, around)], axis=dim)
        done.append(dim)
    return shard


def split_up(shard, dim, devices):
    before, after = (shard.shape[:dim], shard.shape[dim + 1 :])
    return jnp.moveaxis(shard.reshape(*before, devices, -1, *after), dim, 0)


def summed_on_arrival(shard, axis, dim):
    devices = lax.axis_size(axis)
    tiles = lax.all_to_all(split_up(shard, dim, devices), axis, 0, 0, tiled=True)
    return jnp.sum(tiles, axis=0)


def one_axis_at_a_time(shard, axes):
    return functools.reduce(lax.psum, axes, shard)


def advance(current_estimate, padded, ghost_row, diffusion, velocity, active_cells):
    below = jnp.concatenate([ghost_row[:, :, None], current_estimate[:, :, :-1]], axis=2)
    above = jnp.concatenate(
        [current_estimate[:, :, 1:], jnp.zeros_like(current_estimate[:, :, :1])], axis=2
    )
    couples = (
        (padded[:-2, 1:-1], padded[2:, 1:-1]),
        (padded[1:-1, :-2], padded[1:-1, 2:]),
        (below, above),
    )
    spread = -6.0 * current_estimate
    carried = jnp.zeros_like(current_estimate)
    for component in range(3):
        behind, ahead = couples[component]
        spread = spread + behind + ahead
        flow_speed = velocity[component]
        carried = (
            carried
            + jnp.maximum(flow_speed, 0.0) * (current_estimate - behind)
            + jnp.minimum(flow_speed, 0.0) * (ahead - current_estimate)
        )
    return current_estimate + active_cells * (diffusion * spread - carried)


def neighbours(field, padded):
    below = jnp.concatenate([jnp.zeros_like(field[:, :, :1]), field[:, :, :-1]], axis=2)
    above = jnp.concatenate([field[:, :, 1:], jnp.zeros_like(field[:, :, :1])], axis=2)
    return (padded[:-2, 1:-1], padded[2:, 1:-1], padded[1:-1, :-2], padded[1:-1, 2:], below, above)


def thermal_flow_operator(field, padded_field, thermal_conductance, bordered_conductance, capacity):
    accumulated = capacity * field
    for near_value, near_cond in zip(
        neighbours(field, padded_field), neighbours(thermal_conductance, bordered_conductance)
    ):
        accumulated = accumulated + 0.5 * (thermal_conductance + near_cond) * (field - near_value)
    return accumulated


def diagonal_of(thermal_conductance, bordered_conductance, capacity):
    accumulated = capacity
    for near_cond in neighbours(thermal_conductance, bordered_conductance):
        accumulated = accumulated + 0.5 * (thermal_conductance + near_cond)
    return accumulated


def local(
    liquid_starting_warmth,
    liquid_spreading_ratios,
    liquid_advective_ratios,
    liquid_refresh_flags,
    wall_starting_warmth,
    wall_thermal_capacity,
    thermal_conductance,
    wall_energy_output,
    coupling_partner_lookup,
):
    topmost_layers = gathered_copies(wall_starting_warmth[:, :, -1], GY, 1)
    positions = jnp.arange(topmost_layers.shape[1], dtype=jnp.int32)
    picks = coupling_partner_lookup[:, :, None] == positions[None, None, :]
    ghost_row = jnp.sum(jnp.where(picks, topmost_layers[:, None, :], 0.0), axis=2)
    active_cells = jnp.repeat(liquid_refresh_flags.astype(jnp.float32), ZB, axis=2)
    padded_fluid, bordered_wall_warmth, bordered_conductance = (
        with_halo(liquid_starting_warmth, ((GX, 0), (GY, 1)), 1),
        with_halo(wall_starting_warmth, ((GX, 0), (GY, 1)), 1),
        with_halo(thermal_conductance, ((GX, 0), (GY, 1)), 1),
    )
    current_estimate = liquid_starting_warmth
    padded = padded_fluid
    flux_sum = jnp.zeros_like(ghost_row)
    for substep in range(SUBSTEPS):
        flux_sum = flux_sum + (current_estimate[:, :, 0] - ghost_row)
        if substep > 0:
            padded = with_halo(current_estimate, ((GX, 0), (GY, 1)), 1)
        current_estimate = advance(
            current_estimate,
            padded,
            ghost_row,
            liquid_spreading_ratios,
            liquid_advective_ratios,
            active_cells,
        )
    flux_mean = flux_sum / SUBSTEPS
    placed = jnp.sum(jnp.where(picks, flux_mean[:, :, None], 0.0), axis=1)
    arrived = summed_on_arrival(placed, GY, 1)
    equation_source_term = wall_thermal_capacity * wall_starting_warmth + wall_energy_output
    equation_source_term = equation_source_term.at[:, :, -1].add(arrived)
    diagonal = diagonal_of(thermal_conductance, bordered_conductance, wall_thermal_capacity)

    def apply_stiffness_matrix(field, padded_field):
        return thermal_flow_operator(
            field, padded_field, thermal_conductance, bordered_conductance, wall_thermal_capacity
        )

    def rimmed(field):
        return with_halo(field, ((GX, 0), (GY, 1)), 1)

    converged_warmth = wall_starting_warmth
    leftover_error = equation_source_term - apply_stiffness_matrix(
        converged_warmth, bordered_wall_warmth
    )
    scaled = leftover_error / diagonal

    def paired(residual_now, scaled_now, image_now):
        return (
            one_axis_at_a_time(jnp.sum(residual_now * scaled_now), GX_GY),
            one_axis_at_a_time(jnp.sum(scaled_now * image_now), GX_GY),
        )

    image = apply_stiffness_matrix(scaled, rimmed(scaled))
    inner_rz, curvature = paired(leftover_error, scaled, image)
    descent_length = inner_rz / curvature
    search_heading = scaled
    image_dir = image
    for iteration in range(ITERS):
        converged_warmth = converged_warmth + descent_length * search_heading
        leftover_error = leftover_error - descent_length * image_dir
        if iteration + 1 < ITERS:
            scaled = leftover_error / diagonal
            image = apply_stiffness_matrix(scaled, rimmed(scaled))
            inner_next, curvature = paired(leftover_error, scaled, image)
            ratio = inner_next / inner_rz
            descent_length = inner_next / (curvature - ratio * inner_next / descent_length)
            search_heading = scaled + ratio * search_heading
            image_dir = image + ratio * image_dir
            inner_rz = inner_next
    return (current_estimate, converged_warmth)


def solution(mesh):
    finer = Mesh(mesh.devices.reshape(4, 4, 2, 4, 2), ("gx_0", "gx_1", "gy_0", "gy_1", "gy_2"))
    in_specs = (
        P(GX, GY, None),
        P(GX, GY, None),
        P(None, GX, GY, None),
        P(GX, GY, None),
        P(GX, GY, None),
        P(GX, GY, None),
        P(GX, GY, None),
        P(GX, GY, None),
        P(GX, GY),
    )
    out_specs = (P(GX, GY, None), P(GX, GY, None))
    return jax.shard_map(local, mesh=finer, in_specs=in_specs, out_specs=out_specs, check_vma=False)
```

profile of v0, /device:TPU:1, one launch (start us, length us, event | category | flops | bytes accessed | tf_op | source)
XLA Modules:
  0.0 388.2 jit_solution(8519919748444019785)
XLA Ops:
  2.2 7.2 %all-to-all-start = ((f32[16,4,16]{2,1,0:T(4,128)}), f32[16,4,16]{2,1,0:T(4,128)S(1)}, u32[]{:S(2)}, u32[]{:S(2)}) async-start(f32[16,4,16]{2,1,0:T(4,128)} %broadcast_in_dim.42), calls=%async_computation | async-start | bytes 65536 | tf_op jit(solution)/shard_map/all_to_all | solution.py:25
  12.4 3.7 collective-permute-start.2
  19.1 3.6 collective-permute-start.21
  28.8 2.5 collective-permute-start.22
  31.4 4.9 %collective-permute-start = (f32[1,16,1024]{2,1,0:T(8,128)S(1)}, f32[1,16,1024]{2,1,0:T(8,128)S(1)}, u32[]{:S(2)}, u32[]{:S(2)}) collective-permute-start(f32[1,16,1024]{2,1,0:T(8,128)S(1)} %get-tuple-element.146), channel_id=1, source_target_pairs={{0,16},{16,32},{32,48},{48,64},{64,80},{80,96},{96,112},{112,128},... | collective-permute-start | bytes 196616 | tf_op jit(solution)/shard_map/ppermute | solution.py:40
  39.9 6.5 %collective-permute-start.17 = (f32[1,16,1024]{2,1,0:T(8,128)S(1)}, f32[1,16,1024]{2,1,0:T(8,128)S(1)}, u32[]{:S(2)}, u32[]{:S(2)}) collective-permute-start(f32[1,16,1024]{2,1,0:T(8,128)S(1)} %get-tuple-element.117), channel_id=1, source_target_pairs={{0,16},{16,32},{32,48},{48,64},{64,80},{80,96},{96,112},{112,128},... | collective-permute-start | bytes 196616 | tf_op jit(solution)/shard_map/ppermute | solution.py:40
  47.0 5.5 %collective-permute-start.16 = (f32[1,16,1024]{2,1,0:T(8,128)S(1)}, f32[1,16,1024]{2,1,0:T(8,128)S(1)}, u32[]{:S(2)}, u32[]{:S(2)}) collective-permute-start(f32[1,16,1024]{2,1,0:T(8,128)S(1)} %get-tuple-element.122), channel_id=1, source_target_pairs={{0,16},{16,32},{32,48},{48,64},{64,80},{80,96},{96,112},{112,128},... | collective-permute-start | bytes 196616 | tf_op jit(solution)/shard_map/ppermute | solution.py:40
  55.9 2.5 collective-permute-start.7
  58.5 3.8 collective-permute-start.6
  62.4 5.2 %collective-permute-start.4 = (f32[1,16,1024]{2,1,0:T(8,128)S(1)}, f32[1,16,1024]{2,1,0:T(8,128)S(1)}, u32[]{:S(2)}, u32[]{:S(2)}) collective-permute-start(f32[1,16,1024]{2,1,0:T(8,128)S(1)} %get-tuple-element.140), channel_id=1, source_target_pairs={{0,16},{16,32},{32,48},{48,64},{64,80},{80,96},{96,112},{112,128},... | collective-permute-start | bytes 196616 | tf_op jit(solution)/shard_map/ppermute | solution.py:40
  69.7 5.3 %collective-permute-done.5 = f32[1,16,1024]{2,1,0:T(8,128)S(1)} collective-permute-done((f32[1,16,1024]{2,1,0:T(8,128)S(1)}, f32[1,16,1024]{2,1,0:T(8,128)S(1)}, u32[]{:S(2)}, u32[]{:S(2)}) %collective-permute-start.5) | collective-permute-done | bytes 65568 | tf_op jit(solution)/shard_map/ppermute | solution.py:41
  77.4 4.0 %collective-permute-start.10 = (f32[4,1,1024]{2,0,1:T(4,128)S(1)}, f32[4,1,1024]{2,0,1:T(4,128)S(1)}, u32[]{:S(2)}, u32[]{:S(2)}) collective-permute-start(f32[4,1,1024]{2,0,1:T(4,128)S(1)} %copy.858), channel_id=1, source_target_pairs={{0,1},{1,2},{2,3},{3,4},{4,5},{5,6},{6,7},{7,8},{8,9},{9,10},{10,1... | collective-permute-start | bytes 49160 | tf_op jit(solution)/shard_map/ppermute | solution.py:40
  81.4 6.9 %collective-permute-start.8 = (f32[1,16,1024]{2,1,0:T(8,128)S(1)}, f32[1,16,1024]{2,1,0:T(8,128)S(1)}, u32[]{:S(2)}, u32[]{:S(2)}) collective-permute-start(f32[1,16,1024]{2,1,0:T(8,128)S(1)} %get-tuple-element.134), channel_id=1, source_target_pairs={{0,16},{16,32},{32,48},{48,64},{64,80},{80,96},{96,112},{112,128},... | collective-permute-start | bytes 196616 | tf_op jit(solution)/shard_map/ppermute | solution.py:40
  89.9 4.4 %collective-permute-done.9 = f32[1,16,1024]{2,1,0:T(8,128)S(1)} collective-permute-done((f32[1,16,1024]{2,1,0:T(8,128)S(1)}, f32[1,16,1024]{2,1,0:T(8,128)S(1)}, u32[]{:S(2)}, u32[]{:S(2)}) %collective-permute-start.9) | collective-permute-done | bytes 65568 | tf_op jit(solution)/shard_map/ppermute | solution.py:41
  97.1 10.9 %all-to-all-start.1 = ((f32[16,4,16]{2,1,0:T(4,128)}), f32[16,4,16]{2,1,0:T(4,128)S(1)}, u32[]{:S(2)}, u32[]{:S(2)}) async-start(f32[16,4,16]{2,1,0:T(4,128)} %copy.872), calls=%async_computation.1 | async-start | bytes 65536 | tf_op jit(solution)/shard_map/all_to_all | solution.py:59
  111.3 3.5 collective-permute-start.14
  114.8 3.8 collective-permute-start.12
  121.2 2.8 fusion.193
  126.2 3.6 collective-permute-start.26
  130.7 4.9 %collective-permute-start.24 = (f32[1,16,1024]{2,1,0:T(8,128)S(1)}, f32[1,16,1024]{2,1,0:T(8,128)S(1)}, u32[]{:S(2)}, u32[]{:S(2)}) collective-permute-start(f32[1,16,1024]{2,1,0:T(8,128)S(1)} %get-tuple-element.106), channel_id=1, source_target_pairs={{0,16},{16,32},{32,48},{48,64},{64,80},{80,96},{96,112},{112,128},... | collective-permute-start | bytes 196616 | tf_op jit(solution)/shard_map/ppermute | solution.py:40
  139.7 3.1 collective-permute-done.25
  143.8 11.7 %all-reduce.47 = (f32[]{:T(128)}, f32[]{:T(128)}) all-reduce(f32[]{:T(128)} %get-tuple-element.29, f32[]{:T(128)} %get-tuple-element.28), channel_id=1, replica_groups=mesh['gx_0'=4,'gx_1'=4,'gy_0'=2,'gy_1'=4,'gy_2'=2] {'gx_0'}, use_global_device_ids=true, to_apply=%region_4.5 | all-reduce | flops 2 | bytes 16 | tf_op jit(solution)/shard_map/psum | solution.py:64
  155.5 10.3 %all-reduce.43 = (f32[]{:T(128)}, f32[]{:T(128)}) all-reduce(f32[]{:T(128)} %get-tuple-element.52, f32[]{:T(128)} %get-tuple-element.53), channel_id=1, replica_groups=mesh['gx_0'=4,'gx_1'=4,'gy_0'=2,'gy_1'=4,'gy_2'=2] {'gx_1'}, use_global_device_ids=true, to_apply=%region_5.6 | all-reduce | flops 2 | bytes 16 | tf_op jit(solution)/shard_map/psum | solution.py:64
  165.8 4.4 %all-reduce.55 = (f32[]{:T(128)}, f32[]{:T(128)}) all-reduce(f32[]{:T(128)} %get-tuple-element.44, f32[]{:T(128)} %get-tuple-element.45), channel_id=1, replica_groups=mesh['gx_0'=4,'gx_1'=4,'gy_0'=2,'gy_1'=4,'gy_2'=2] {'gy_0'}, use_global_device_ids=true, to_apply=%region_6.7 | all-reduce | flops 2 | bytes 16 | tf_op jit(solution)/shard_map/psum | solution.py:64
  170.2 13.2 %all-reduce.39 = (f32[]{:T(128)}, f32[]{:T(128)}) all-reduce(f32[]{:T(128)} %get-tuple-element.68, f32[]{:T(128)} %get-tuple-element.69), channel_id=1, replica_groups=mesh['gx_0'=4,'gx_1'=4,'gy_0'=2,'gy_1'=4,'gy_2'=2] {'gy_1'}, use_global_device_ids=true, to_apply=%region_7.8 | all-reduce | flops 2 | bytes 16 | tf_op jit(solution)/shard_map/psum | solution.py:64
  183.4 8.1 %all-reduce.51 = (f32[]{:T(128)}, f32[]{:T(128)}) all-reduce(f32[]{:T(128)} %get-tuple-element.36, f32[]{:T(128)} %get-tuple-element.37), channel_id=1, replica_groups=mesh['gx_0'=4,'gx_1'=4,'gy_0'=2,'gy_1'=4,'gy_2'=2] {'gy_2'}, use_global_device_ids=true, to_apply=%region_8.9 | all-reduce | flops 2 | bytes 16 | tf_op jit(solution)/shard_map/psum | solution.py:64
  196.1 3.3 collective-permute-start.30
  202.2 6.7 %collective-permute-done.29 = f32[1,16,1024]{2,1,0:T(8,128)S(1)} collective-permute-done((f32[1,16,1024]{2,1,0:T(8,128)S(1)}, f32[1,16,1024]{2,1,0:T(8,128)S(1)}, u32[]{:S(2)}, u32[]{:S(2)}) %collective-permute-start.29) | collective-permute-done | bytes 65568 | tf_op jit(solution)/shard_map/ppermute | solution.py:41
  210.6 9.4 %all-reduce.46 = (f32[]{:T(128)}, f32[]{:T(128)}) all-reduce(f32[]{:T(128)} %get-tuple-element.27, f32[]{:T(128)} %get-tuple-element.26), channel_id=1, replica_groups=mesh['gx_0'=4,'gx_1'=4,'gy_0'=2,'gy_1'=4,'gy_2'=2] {'gx_0'}, use_global_device_ids=true, to_apply=%region_16.17 | all-reduce | flops 2 | bytes 16 | tf_op jit(solution)/shard_map/psum | solution.py:64
  220.0 11.2 %all-reduce.42 = (f32[]{:T(128)}, f32[]{:T(128)}) all-reduce(f32[]{:T(128)} %get-tuple-element.50, f32[]{:T(128)} %get-tuple-element.51), channel_id=1, replica_groups=mesh['gx_0'=4,'gx_1'=4,'gy_0'=2,'gy_1'=4,'gy_2'=2] {'gx_1'}, use_global_device_ids=true, to_apply=%region_17.18 | all-reduce | flops 2 | bytes 16 | tf_op jit(solution)/shard_map/psum | solution.py:64
  231.2 4.5 %all-reduce.54 = (f32[]{:T(128)}, f32[]{:T(128)}) all-reduce(f32[]{:T(128)} %get-tuple-element.42, f32[]{:T(128)} %get-tuple-element.43), channel_id=1, replica_groups=mesh['gx_0'=4,'gx_1'=4,'gy_0'=2,'gy_1'=4,'gy_2'=2] {'gy_0'}, use_global_device_ids=true, to_apply=%region_18.19 | all-reduce | flops 2 | bytes 16 | tf_op jit(solution)/shard_map/psum | solution.py:64
  235.7 7.3 %all-reduce.38 = (f32[]{:T(128)}, f32[]{:T(128)}) all-reduce(f32[]{:T(128)} %get-tuple-element.66, f32[]{:T(128)} %get-tuple-element.67), channel_id=1, replica_groups=mesh['gx_0'=4,'gx_1'=4,'gy_0'=2,'gy_1'=4,'gy_2'=2] {'gy_1'}, use_global_device_ids=true, to_apply=%region_19.20 | all-reduce | flops 2 | bytes 16 | tf_op jit(solution)/shard_map/psum | solution.py:64
  243.0 9.2 %all-reduce.50 = (f32[]{:T(128)}, f32[]{:T(128)}) all-reduce(f32[]{:T(128)} %get-tuple-element.34, f32[]{:T(128)} %get-tuple-element.35), channel_id=1, replica_groups=mesh['gx_0'=4,'gx_1'=4,'gy_0'=2,'gy_1'=4,'gy_2'=2] {'gy_2'}, use_global_device_ids=true, to_apply=%region_20.21 | all-reduce | flops 2 | bytes 16 | tf_op jit(solution)/shard_map/psum | solution.py:64
  257.7 2.3 collective-permute-start.35
  260.0 3.5 collective-permute-start.34
  266.4 5.1 %collective-permute-done.33 = f32[1,16,1024]{2,1,0:T(8,128)S(1)} collective-permute-done((f32[1,16,1024]{2,1,0:T(8,128)S(1)}, f32[1,16,1024]{2,1,0:T(8,128)S(1)}, u32[]{:S(2)}, u32[]{:S(2)}) %collective-permute-start.33) | collective-permute-done | bytes 65568 | tf_op jit(solution)/shard_map/ppermute | solution.py:41
  273.1 10.2 %all-reduce.45 = (f32[]{:T(128)}, f32[]{:T(128)}) all-reduce(f32[]{:T(128)} %get-tuple-element.25, f32[]{:T(128)} %get-tuple-element.24), channel_id=1, replica_groups=mesh['gx_0'=4,'gx_1'=4,'gy_0'=2,'gy_1'=4,'gy_2'=2] {'gx_0'}, use_global_device_ids=true, to_apply=%region_28.29 | all-reduce | flops 2 | bytes 16 | tf_op jit(solution)/shard_map/psum | solution.py:64
  283.3 11.4 %all-reduce.41 = (f32[]{:T(128)}, f32[]{:T(128)}) all-reduce(f32[]{:T(128)} %get-tuple-element.48, f32[]{:T(128)} %get-tuple-element.49), channel_id=1, replica_groups=mesh['gx_0'=4,'gx_1'=4,'gy_0'=2,'gy_1'=4,'gy_2'=2] {'gx_1'}, use_global_device_ids=true, to_apply=%region_29.30 | all-reduce | flops 2 | bytes 16 | tf_op jit(solution)/shard_map/psum | solution.py:64
  294.7 4.5 %all-reduce.53 = (f32[]{:T(128)}, f32[]{:T(128)}) all-reduce(f32[]{:T(128)} %get-tuple-element.40, f32[]{:T(128)} %get-tuple-element.41), channel_id=1, replica_groups=mesh['gx_0'=4,'gx_1'=4,'gy_0'=2,'gy_1'=4,'gy_2'=2] {'gy_0'}, use_global_device_ids=true, to_apply=%region_30.31 | all-reduce | flops 2 | bytes 16 | tf_op jit(solution)/shard_map/psum | solution.py:64
  299.2 10.1 %all-reduce.37 = (f32[]{:T(128)}, f32[]{:T(128)}) all-reduce(f32[]{:T(128)} %get-tuple-element.64, f32[]{:T(128)} %get-tuple-element.65), channel_id=1, replica_groups=mesh['gx_0'=4,'gx_1'=4,'gy_0'=2,'gy_1'=4,'gy_2'=2] {'gy_1'}, use_global_device_ids=true, to_apply=%region_31.32 | all-reduce | flops 2 | bytes 16 | tf_op jit(solution)/shard_map/psum | solution.py:64
  309.2 10.0 %all-reduce.49 = (f32[]{:T(128)}, f32[]{:T(128)}) all-reduce(f32[]{:T(128)} %get-tuple-element.32, f32[]{:T(128)} %get-tuple-element.33), channel_id=1, replica_groups=mesh['gx_0'=4,'gx_1'=4,'gy_0'=2,'gy_1'=4,'gy_2'=2] {'gy_2'}, use_global_device_ids=true, to_apply=%region_32.33 | all-reduce | flops 2 | bytes 16 | tf_op jit(solution)/shard_map/psum | solution.py:64
  327.3 3.3 collective-permute-start.38
  333.4 6.9 %collective-permute-done.37 = f32[1,16,1024]{2,1,0:T(8,128)S(1)} collective-permute-done((f32[1,16,1024]{2,1,0:T(8,128)S(1)}, f32[1,16,1024]{2,1,0:T(8,128)S(1)}, u32[]{:S(2)}, u32[]{:S(2)}) %collective-permute-start.37) | collective-permute-done | bytes 65568 | tf_op jit(solution)/shard_map/ppermute | solution.py:41
  341.2 10.1 %all-reduce.44 = (f32[]{:T(128)}, f32[]{:T(128)}) all-reduce(f32[]{:T(128)} %get-tuple-element.70, f32[]{:T(128)} %fusion.182), channel_id=1, replica_groups=mesh['gx_0'=4,'gx_1'=4,'gy_0'=2,'gy_1'=4,'gy_2'=2] {'gx_0'}, use_global_device_ids=true, to_apply=%region_40.41 | all-reduce | flops 2 | bytes 16 | tf_op jit(solution)/shard_map/psum | solution.py:64
  351.3 11.6 %all-reduce.40 = (f32[]{:T(128)}, f32[]{:T(128)}) all-reduce(f32[]{:T(128)} %get-tuple-element.46, f32[]{:T(128)} %get-tuple-element.47), channel_id=1, replica_groups=mesh['gx_0'=4,'gx_1'=4,'gy_0'=2,'gy_1'=4,'gy_2'=2] {'gx_1'}, use_global_device_ids=true, to_apply=%region_41.42 | all-reduce | flops 2 | bytes 16 | tf_op jit(solution)/shard_map/psum | solution.py:64
  362.9 4.4 %all-reduce.52 = (f32[]{:T(128)}, f32[]{:T(128)}) all-reduce(f32[]{:T(128)} %get-tuple-element.38, f32[]{:T(128)} %get-tuple-element.39), channel_id=1, replica_groups=mesh['gx_0'=4,'gx_1'=4,'gy_0'=2,'gy_1'=4,'gy_2'=2] {'gy_0'}, use_global_device_ids=true, to_apply=%region_42.43 | all-reduce | flops 2 | bytes 16 | tf_op jit(solution)/shard_map/psum | solution.py:64
  367.2 6.7 %all-reduce.36 = (f32[]{:T(128)}, f32[]{:T(128)}) all-reduce(f32[]{:T(128)} %get-tuple-element.62, f32[]{:T(128)} %get-tuple-element.63), channel_id=1, replica_groups=mesh['gx_0'=4,'gx_1'=4,'gy_0'=2,'gy_1'=4,'gy_2'=2] {'gy_1'}, use_global_device_ids=true, to_apply=%region_43.44 | all-reduce | flops 2 | bytes 16 | tf_op jit(solution)/shard_map/psum | solution.py:64
  373.9 9.6 %all-reduce.48 = (f32[]{:T(128)}, f32[]{:T(128)}) all-reduce(f32[]{:T(128)} %get-tuple-element.30, f32[]{:T(128)} %get-tuple-element.31), channel_id=1, replica_groups=mesh['gx_0'=4,'gx_1'=4,'gy_0'=2,'gy_1'=4,'gy_2'=2] {'gy_2'}, use_global_device_ids=true, to_apply=%region_44.45 | all-reduce | flops 2 | bytes 16 | tf_op jit(solution)/shard_map/psum | solution.py:64
  (212 shorter events, 65.5 us)
Async XLA Ops:
  0.6 22.1 %copy-start = (f32[4,16,1024]{2,1,0:T(8,128)S(1)}, f32[4,16,1024]{2,1,0:T(8,128)}, u32[]{:S(2)}) copy-start(f32[4,16,1024]{2,1,0:T(8,128)} %param.17) | copy-start | bytes 786436
  2.2 26.5 %all-to-all-start = ((f32[16,4,16]{2,1,0:T(4,128)}), f32[16,4,16]{2,1,0:T(4,128)S(1)}, u32[]{:S(2)}, u32[]{:S(2)}) async-start(f32[16,4,16]{2,1,0:T(4,128)} %broadcast_in_dim.42), calls=%async_computation | async-start | bytes 65536 | tf_op jit(solution)/shard_map/all_to_all | solution.py:25
  10.4 18.4 %collective-permute-start.3 = (f32[4,1,1024]{2,0,1:T(4,128)S(1)}, f32[4,1,1024]{2,0,1:T(4,128)S(1)}, u32[]{:S(2)}, u32[]{:S(2)}) collective-permute-start(f32[4,1,1024]{2,0,1:T(4,128)S(1)} %copy.899), channel_id=1, source_target_pairs={{1,0},{2,1},{3,2},{4,3},{5,4},{6,5},{7,6},{8,7},{9,8},{10,9},{11,1... | collective-permute-start | bytes 49160 | tf_op jit(solution)/shard_map/ppermute | solution.py:41
  12.4 18.9 %collective-permute-start.2 = (f32[4,1,1024]{2,0,1:T(4,128)S(1)}, f32[4,1,1024]{2,0,1:T(4,128)S(1)}, u32[]{:S(2)}, u32[]{:S(2)}) collective-permute-start(f32[4,1,1024]{2,0,1:T(4,128)S(1)} %copy.898), channel_id=1, source_target_pairs={{0,1},{1,2},{2,3},{3,4},{4,5},{5,6},{6,7},{7,8},{8,9},{9,10},{10,1... | collective-permute-start | bytes 49160 | tf_op jit(solution)/shard_map/ppermute | solution.py:40
  17.1 19.5 %collective-permute-start.23 = (f32[4,1,1024]{2,0,1:T(4,128)S(1)}, f32[4,1,1024]{2,0,1:T(4,128)S(1)}, u32[]{:S(2)}, u32[]{:S(2)}) collective-permute-start(f32[4,1,1024]{2,0,1:T(4,128)S(1)} %copy.903), channel_id=1, source_target_pairs={{1,0},{2,1},{3,2},{4,3},{5,4},{6,5},{7,6},{8,7},{9,8},{10,9},{11,1... | collective-permute-start | bytes 49160 | tf_op jit(solution)/shard_map/ppermute | solution.py:41
  19.1 18.9 %collective-permute-start.21 = (f32[4,1,1024]{2,0,1:T(4,128)S(1)}, f32[4,1,1024]{2,0,1:T(4,128)S(1)}, u32[]{:S(2)}, u32[]{:S(2)}) collective-permute-start(f32[4,1,1024]{2,0,1:T(4,128)S(1)} %copy.901), channel_id=1, source_target_pairs={{0,1},{1,2},{2,3},{3,4},{4,5},{5,6},{6,7},{7,8},{8,9},{9,10},{10,1... | collective-permute-start | bytes 49160 | tf_op jit(solution)/shard_map/ppermute | solution.py:40
  22.8 17.1 %collective-permute-start.20 = (f32[4,1,1024]{2,0,1:T(4,128)S(1)}, f32[4,1,1024]{2,0,1:T(4,128)S(1)}, u32[]{:S(2)}, u32[]{:S(2)}) collective-permute-start(f32[4,1,1024]{2,0,1:T(4,128)S(1)} %copy.900), channel_id=1, source_target_pairs={{0,1},{1,2},{2,3},{3,4},{4,5},{5,6},{6,7},{7,8},{8,9},{9,10},{10,1... | collective-permute-start | bytes 49160 | tf_op jit(solution)/shard_map/ppermute | solution.py:40
  28.7 25.8 %copy-start.1 = (f32[3,4,16,1024]{3,2,1,0:T(8,128)S(1)}, f32[3,4,16,1024]{3,2,1,0:T(8,128)}, u32[]{:S(2)}) copy-start(f32[3,4,16,1024]{3,2,1,0:T(8,128)} %param.13) | copy-start | bytes 2359300
  28.8 18.1 %collective-permute-start.22 = (f32[4,1,1024]{2,0,1:T(4,128)S(1)}, f32[4,1,1024]{2,0,1:T(4,128)S(1)}, u32[]{:S(2)}, u32[]{:S(2)}) collective-permute-start(f32[4,1,1024]{2,0,1:T(4,128)S(1)} %copy.902), channel_id=1, source_target_pairs={{1,0},{2,1},{3,2},{4,3},{5,4},{6,5},{7,6},{8,7},{9,8},{10,9},{11,1... | collective-permute-start | bytes 49160 | tf_op jit(solution)/shard_map/ppermute | solution.py:41
  31.4 21.7 %collective-permute-start = (f32[1,16,1024]{2,1,0:T(8,128)S(1)}, f32[1,16,1024]{2,1,0:T(8,128)S(1)}, u32[]{:S(2)}, u32[]{:S(2)}) collective-permute-start(f32[1,16,1024]{2,1,0:T(8,128)S(1)} %get-tuple-element.146), channel_id=1, source_target_pairs={{0,16},{16,32},{32,48},{48,64},{64,80},{80,96},{96,112},{112,128},... | collective-permute-start | bytes 196616 | tf_op jit(solution)/shard_map/ppermute | solution.py:40
  36.6 58.1 %copy-start.11 = (f32[4,16,1]{2,1,0:T(8,128)}, f32[4,16,1]{2,1,0:T(8,128)S(1)}, u32[]{:S(2)}) copy-start(f32[4,16,1]{2,1,0:T(8,128)S(1)} %copy.852) | copy-start | bytes 772
  36.6 17.8 %collective-permute-start.1 = (f32[1,16,1024]{2,1,0:T(8,128)S(1)}, f32[1,16,1024]{2,1,0:T(8,128)S(1)}, u32[]{:S(2)}, u32[]{:S(2)}) collective-permute-start(f32[1,16,1024]{2,1,0:T(8,128)S(1)} %get-tuple-element.147), channel_id=1, source_target_pairs={{16,0},{32,16},{48,32},{64,48},{80,64},{96,80},{112,96},{128,112},... | collective-permute-start | bytes 196616 | tf_op jit(solution)/shard_map/ppermute | solution.py:41
  38.0 31.0 %collective-permute-start.19 = (f32[1,16,1024]{2,1,0:T(8,128)S(1)}, f32[1,16,1024]{2,1,0:T(8,128)S(1)}, u32[]{:S(2)}, u32[]{:S(2)}) collective-permute-start(f32[1,16,1024]{2,1,0:T(8,128)S(1)} %get-tuple-element.116), channel_id=1, source_target_pairs={{16,0},{32,16},{48,32},{64,48},{80,64},{96,80},{112,96},{128,112},... | collective-permute-start | bytes 196616 | tf_op jit(solution)/shard_map/ppermute | solution.py:41
  39.9 18.6 %collective-permute-start.17 = (f32[1,16,1024]{2,1,0:T(8,128)S(1)}, f32[1,16,1024]{2,1,0:T(8,128)S(1)}, u32[]{:S(2)}, u32[]{:S(2)}) collective-permute-start(f32[1,16,1024]{2,1,0:T(8,128)S(1)} %get-tuple-element.117), channel_id=1, source_target_pairs={{0,16},{16,32},{32,48},{48,64},{64,80},{80,96},{96,112},{112,128},... | collective-permute-start | bytes 196616 | tf_op jit(solution)/shard_map/ppermute | solution.py:40
  47.0 15.4 %collective-permute-start.16 = (f32[1,16,1024]{2,1,0:T(8,128)S(1)}, f32[1,16,1024]{2,1,0:T(8,128)S(1)}, u32[]{:S(2)}, u32[]{:S(2)}) collective-permute-start(f32[1,16,1024]{2,1,0:T(8,128)S(1)} %get-tuple-element.122), channel_id=1, source_target_pairs={{0,16},{16,32},{32,48},{48,64},{64,80},{80,96},{96,112},{112,128},... | collective-permute-start | bytes 196616 | tf_op jit(solution)/shard_map/ppermute | solution.py:40
  53.0 14.6 %collective-permute-start.18 = (f32[1,16,1024]{2,1,0:T(8,128)S(1)}, f32[1,16,1024]{2,1,0:T(8,128)S(1)}, u32[]{:S(2)}, u32[]{:S(2)}) collective-permute-start(f32[1,16,1024]{2,1,0:T(8,128)S(1)} %get-tuple-element.123), channel_id=1, source_target_pairs={{16,0},{32,16},{48,32},{64,48},{80,64},{96,80},{112,96},{128,112},... | collective-permute-start | bytes 196616 | tf_op jit(solution)/shard_map/ppermute | solution.py:41
  55.9 13.7 %collective-permute-start.7 = (f32[4,1,1024]{2,0,1:T(4,128)S(1)}, f32[4,1,1024]{2,0,1:T(4,128)S(1)}, u32[]{:S(2)}, u32[]{:S(2)}) collective-permute-start(f32[4,1,1024]{2,0,1:T(4,128)S(1)} %copy.855), channel_id=1, source_target_pairs={{1,0},{2,1},{3,2},{4,3},{5,4},{6,5},{7,6},{8,7},{9,8},{10,9},{11,1... | collective-permute-start | bytes 49160 | tf_op jit(solution)/shard_map/ppermute | solution.py:41
  58.5 11.2 %collective-permute-start.6 = (f32[4,1,1024]{2,0,1:T(4,128)S(1)}, f32[4,1,1024]{2,0,1:T(4,128)S(1)}, u32[]{:S(2)}, u32[]{:S(2)}) collective-permute-start(f32[4,1,1024]{2,0,1:T(4,128)S(1)} %copy.853), channel_id=1, source_target_pairs={{0,1},{1,2},{2,3},{3,4},{4,5},{5,6},{6,7},{7,8},{8,9},{9,10},{10,1... | collective-permute-start | bytes 49160 | tf_op jit(solution)/shard_map/ppermute | solution.py:40
  62.4 7.3 %collective-permute-start.4 = (f32[1,16,1024]{2,1,0:T(8,128)S(1)}, f32[1,16,1024]{2,1,0:T(8,128)S(1)}, u32[]{:S(2)}, u32[]{:S(2)}) collective-permute-start(f32[1,16,1024]{2,1,0:T(8,128)S(1)} %get-tuple-element.140), channel_id=1, source_target_pairs={{0,16},{16,32},{32,48},{48,64},{64,80},{80,96},{96,112},{112,128},... | collective-permute-start | bytes 196616 | tf_op jit(solution)/shard_map/ppermute | solution.py:40
  67.6 7.4 %collective-permute-start.5 = (f32[1,16,1024]{2,1,0:T(8,128)S(1)}, f32[1,16,1024]{2,1,0:T(8,128)S(1)}, u32[]{:S(2)}, u32[]{:S(2)}) collective-permute-start(f32[1,16,1024]{2,1,0:T(8,128)S(1)} %get-tuple-element.141), channel_id=1, source_target_pairs={{16,0},{32,16},{48,32},{64,48},{80,64},{96,80},{112,96},{128,112},... | collective-permute-start | bytes 196616 | tf_op jit(solution)/shard_map/ppermute | solution.py:41
  75.5 14.3 %collective-permute-start.11 = (f32[4,1,1024]{2,0,1:T(4,128)S(1)}, f32[4,1,1024]{2,0,1:T(4,128)S(1)}, u32[]{:S(2)}, u32[]{:S(2)}) collective-permute-start(f32[4,1,1024]{2,0,1:T(4,128)S(1)} %copy.860), channel_id=1, source_target_pairs={{1,0},{2,1},{3,2},{4,3},{5,4},{6,5},{7,6},{8,7},{9,8},{10,9},{11,1... | collective-permute-start | bytes 49160 | tf_op jit(solution)/shard_map/ppermute | solution.py:41
  77.4 12.4 %collective-permute-start.10 = (f32[4,1,1024]{2,0,1:T(4,128)S(1)}, f32[4,1,1024]{2,0,1:T(4,128)S(1)}, u32[]{:S(2)}, u32[]{:S(2)}) collective-permute-start(f32[4,1,1024]{2,0,1:T(4,128)S(1)} %copy.858), channel_id=1, source_target_pairs={{0,1},{1,2},{2,3},{3,4},{4,5},{5,6},{6,7},{7,8},{8,9},{9,10},{10,1... | collective-permute-start | bytes 49160 | tf_op jit(solution)/shard_map/ppermute | solution.py:40
  81.4 8.4 %collective-permute-start.8 = (f32[1,16,1024]{2,1,0:T(8,128)S(1)}, f32[1,16,1024]{2,1,0:T(8,128)S(1)}, u32[]{:S(2)}, u32[]{:S(2)}) collective-permute-start(f32[1,16,1024]{2,1,0:T(8,128)S(1)} %get-tuple-element.134), channel_id=1, source_target_pairs={{0,16},{16,32},{32,48},{48,64},{64,80},{80,96},{96,112},{112,128},... | collective-permute-start | bytes 196616 | tf_op jit(solution)/shard_map/ppermute | solution.py:40
  88.4 5.9 %collective-permute-start.9 = (f32[1,16,1024]{2,1,0:T(8,128)S(1)}, f32[1,16,1024]{2,1,0:T(8,128)S(1)}, u32[]{:S(2)}, u32[]{:S(2)}) collective-permute-start(f32[1,16,1024]{2,1,0:T(8,128)S(1)} %get-tuple-element.135), channel_id=1, source_target_pairs={{16,0},{32,16},{48,32},{64,48},{80,64},{96,80},{112,96},{128,112},... | collective-permute-start | bytes 196616 | tf_op jit(solution)/shard_map/ppermute | solution.py:41
  97.1 22.8 %all-to-all-start.1 = ((f32[16,4,16]{2,1,0:T(4,128)}), f32[16,4,16]{2,1,0:T(4,128)S(1)}, u32[]{:S(2)}, u32[]{:S(2)}) async-start(f32[16,4,16]{2,1,0:T(4,128)} %copy.872), calls=%async_computation.1 | async-start | bytes 65536 | tf_op jit(solution)/shard_map/all_to_all | solution.py:59
  109.2 17.0 %collective-permute-start.15 = (f32[4,1,1024]{2,0,1:T(4,128)}, f32[4,1,1024]{2,0,1:T(4,128)}, u32[]{:S(2)}, u32[]{:S(2)}) collective-permute-start(f32[4,1,1024]{2,0,1:T(4,128)} %copy.865), channel_id=1, source_target_pairs={{1,0},{2,1},{3,2},{4,3},{5,4},{6,5},{7,6},{8,7},{9,8},{10,9},{11,1... | collective-permute-start | bytes 49160 | tf_op jit(solution)/shard_map/ppermute | solution.py:41
  111.3 19.4 %collective-permute-start.14 = (f32[4,1,1024]{2,0,1:T(4,128)}, f32[4,1,1024]{2,0,1:T(4,128)}, u32[]{:S(2)}, u32[]{:S(2)}) collective-permute-start(f32[4,1,1024]{2,0,1:T(4,128)} %copy.863), channel_id=1, source_target_pairs={{0,1},{1,2},{2,3},{3,4},{4,5},{5,6},{6,7},{7,8},{8,9},{9,10},{10,1... | collective-permute-start | bytes 49160 | tf_op jit(solution)/shard_map/ppermute | solution.py:40
  114.8 22.9 %collective-permute-start.12 = (f32[1,16,1024]{2,1,0:T(8,128)}, f32[1,16,1024]{2,1,0:T(8,128)}, u32[]{:S(2)}, u32[]{:S(2)}) collective-permute-start(f32[1,16,1024]{2,1,0:T(8,128)} %get-tuple-element.128), channel_id=1, source_target_pairs={{0,16},{16,32},{32,48},{48,64},{64,80},{80,96},{96,112},{112,128},... | collective-permute-start | bytes 196616 | tf_op jit(solution)/shard_map/ppermute | solution.py:40
  118.6 19.1 %collective-permute-start.13 = (f32[1,16,1024]{2,1,0:T(8,128)}, f32[1,16,1024]{2,1,0:T(8,128)}, u32[]{:S(2)}, u32[]{:S(2)}) collective-permute-start(f32[1,16,1024]{2,1,0:T(8,128)} %get-tuple-element.129), channel_id=1, source_target_pairs={{16,0},{32,16},{48,32},{64,48},{80,64},{96,80},{112,96},{128,112},... | collective-permute-start | bytes 196616 | tf_op jit(solution)/shard_map/ppermute | solution.py:41
  123.9 18.9 %copy-start.8 = (f32[4,16,1024]{2,1,0:T(8,128)}, f32[4,16,1024]{2,1,0:T(8,128)S(1)}, u32[]{:S(2)}) copy-start(f32[4,16,1024]{2,1,0:T(8,128)S(1)} %get-tuple-element.81) | copy-start | bytes 786436
  124.2 12.1 %collective-permute-start.27 = (f32[4,1,1024]{2,0,1:T(4,128)S(1)}, f32[4,1,1024]{2,0,1:T(4,128)S(1)}, u32[]{:S(2)}, u32[]{:S(2)}) collective-permute-start(f32[4,1,1024]{2,0,1:T(4,128)S(1)} %copy.884), channel_id=1, source_target_pairs={{1,0},{2,1},{3,2},{4,3},{5,4},{6,5},{7,6},{8,7},{9,8},{10,9},{11,1... | collective-permute-start | bytes 49160 | tf_op jit(solution)/shard_map/ppermute | solution.py:41
  126.2 11.4 %collective-permute-start.26 = (f32[4,1,1024]{2,0,1:T(4,128)S(1)}, f32[4,1,1024]{2,0,1:T(4,128)S(1)}, u32[]{:S(2)}, u32[]{:S(2)}) collective-permute-start(f32[4,1,1024]{2,0,1:T(4,128)S(1)} %copy.882), channel_id=1, source_target_pairs={{0,1},{1,2},{2,3},{3,4},{4,5},{5,6},{6,7},{7,8},{8,9},{9,10},{10,1... | collective-permute-start | bytes 49160 | tf_op jit(solution)/shard_map/ppermute | solution.py:40
  130.7 9.1 %collective-permute-start.24 = (f32[1,16,1024]{2,1,0:T(8,128)S(1)}, f32[1,16,1024]{2,1,0:T(8,128)S(1)}, u32[]{:S(2)}, u32[]{:S(2)}) collective-permute-start(f32[1,16,1024]{2,1,0:T(8,128)S(1)} %get-tuple-element.106), channel_id=1, source_target_pairs={{0,16},{16,32},{32,48},{48,64},{64,80},{80,96},{96,112},{112,128},... | collective-permute-start | bytes 196616 | tf_op jit(solution)/shard_map/ppermute | solution.py:40
  136.3 6.5 %collective-permute-start.25 = (f32[1,16,1024]{2,1,0:T(8,128)S(1)}, f32[1,16,1024]{2,1,0:T(8,128)S(1)}, u32[]{:S(2)}, u32[]{:S(2)}) collective-permute-start(f32[1,16,1024]{2,1,0:T(8,128)S(1)} %get-tuple-element.107), channel_id=1, source_target_pairs={{16,0},{32,16},{48,32},{64,48},{80,64},{96,80},{112,96},{128,112},... | collective-permute-start | bytes 196616 | tf_op jit(solution)/shard_map/ppermute | solution.py:41
  142.8 49.9 %copy-start.7 = (f32[4,16,1024]{2,1,0:T(8,128)S(1)}, f32[4,16,1024]{2,1,0:T(8,128)}, u32[]{:S(2)}) copy-start(f32[4,16,1024]{2,1,0:T(8,128)} %get-tuple-element.80) | copy-start | bytes 786436
  193.8 8.3 %collective-permute-start.31 = (f32[4,1,1024]{2,0,1:T(4,128)S(1)}, f32[4,1,1024]{2,0,1:T(4,128)S(1)}, u32[]{:S(2)}, u32[]{:S(2)}) collective-permute-start(f32[4,1,1024]{2,0,1:T(4,128)S(1)} %copy.888), channel_id=1, source_target_pairs={{1,0},{2,1},{3,2},{4,3},{5,4},{6,5},{7,6},{8,7},{9,8},{10,9},{11,1... | collective-permute-start | bytes 49160 | tf_op jit(solution)/shard_map/ppermute | solution.py:41
  196.1 6.1 %collective-permute-start.30 = (f32[4,1,1024]{2,0,1:T(4,128)S(1)}, f32[4,1,1024]{2,0,1:T(4,128)S(1)}, u32[]{:S(2)}, u32[]{:S(2)}) collective-permute-start(f32[4,1,1024]{2,0,1:T(4,128)S(1)} %copy.886), channel_id=1, source_target_pairs={{0,1},{1,2},{2,3},{3,4},{4,5},{5,6},{6,7},{7,8},{8,9},{9,10},{10,1... | collective-permute-start | bytes 49160 | tf_op jit(solution)/shard_map/ppermute | solution.py:40
  199.4 2.8 collective-permute-start.28
  200.7 8.2 %collective-permute-start.29 = (f32[1,16,1024]{2,1,0:T(8,128)S(1)}, f32[1,16,1024]{2,1,0:T(8,128)S(1)}, u32[]{:S(2)}, u32[]{:S(2)}) collective-permute-start(f32[1,16,1024]{2,1,0:T(8,128)S(1)} %get-tuple-element.101), channel_id=1, source_target_pairs={{16,0},{32,16},{48,32},{64,48},{80,64},{96,80},{112,96},{128,112},... | collective-permute-start | bytes 196616 | tf_op jit(solution)/shard_map/ppermute | solution.py:41
  257.7 13.8 %copy-start.9 = (f32[4,16,1024]{2,1,0:T(8,128)}, f32[4,16,1024]{2,1,0:T(8,128)S(1)}, u32[]{:S(2)}) copy-start(f32[4,16,1024]{2,1,0:T(8,128)S(1)} %get-tuple-element.74) | copy-start | bytes 786436
  257.7 8.5 %collective-permute-start.35 = (f32[4,1,1024]{2,0,1:T(4,128)S(1)}, f32[4,1,1024]{2,0,1:T(4,128)S(1)}, u32[]{:S(2)}, u32[]{:S(2)}) collective-permute-start(f32[4,1,1024]{2,0,1:T(4,128)S(1)} %copy.892), channel_id=1, source_target_pairs={{1,0},{2,1},{3,2},{4,3},{5,4},{6,5},{7,6},{8,7},{9,8},{10,9},{11,1... | collective-permute-start | bytes 49160 | tf_op jit(solution)/shard_map/ppermute | solution.py:41
  260.0 6.3 %collective-permute-start.34 = (f32[4,1,1024]{2,0,1:T(4,128)S(1)}, f32[4,1,1024]{2,0,1:T(4,128)S(1)}, u32[]{:S(2)}, u32[]{:S(2)}) collective-permute-start(f32[4,1,1024]{2,0,1:T(4,128)S(1)} %copy.890), channel_id=1, source_target_pairs={{0,1},{1,2},{2,3},{3,4},{4,5},{5,6},{6,7},{7,8},{8,9},{9,10},{10,1... | collective-permute-start | bytes 49160 | tf_op jit(solution)/shard_map/ppermute | solution.py:40
  263.5 2.8 collective-permute-start.32
  264.8 6.6 %collective-permute-start.33 = (f32[1,16,1024]{2,1,0:T(8,128)S(1)}, f32[1,16,1024]{2,1,0:T(8,128)S(1)}, u32[]{:S(2)}, u32[]{:S(2)}) collective-permute-start(f32[1,16,1024]{2,1,0:T(8,128)S(1)} %get-tuple-element.95), channel_id=1, source_target_pairs={{16,0},{32,16},{48,32},{64,48},{80,64},{96,80},{112,96},{128,112},... | collective-permute-start | bytes 196616 | tf_op jit(solution)/shard_map/ppermute | solution.py:41
  325.0 8.3 %collective-permute-start.39 = (f32[4,1,1024]{2,0,1:T(4,128)S(1)}, f32[4,1,1024]{2,0,1:T(4,128)S(1)}, u32[]{:S(2)}, u32[]{:S(2)}) collective-permute-start(f32[4,1,1024]{2,0,1:T(4,128)S(1)} %copy.896), channel_id=1, source_target_pairs={{1,0},{2,1},{3,2},{4,3},{5,4},{6,5},{7,6},{8,7},{9,8},{10,9},{11,1... | collective-permute-start | bytes 49160 | tf_op jit(solution)/shard_map/ppermute | solution.py:41
  327.3 6.1 %collective-permute-start.38 = (f32[4,1,1024]{2,0,1:T(4,128)S(1)}, f32[4,1,1024]{2,0,1:T(4,128)S(1)}, u32[]{:S(2)}, u32[]{:S(2)}) collective-permute-start(f32[4,1,1024]{2,0,1:T(4,128)S(1)} %copy.894), channel_id=1, source_target_pairs={{0,1},{1,2},{2,3},{3,4},{4,5},{5,6},{6,7},{7,8},{8,9},{9,10},{10,1... | collective-permute-start | bytes 49160 | tf_op jit(solution)/shard_map/ppermute | solution.py:40
  330.6 2.8 collective-permute-start.36
  331.9 8.4 %collective-permute-start.37 = (f32[1,16,1024]{2,1,0:T(8,128)S(1)}, f32[1,16,1024]{2,1,0:T(8,128)S(1)}, u32[]{:S(2)}, u32[]{:S(2)}) collective-permute-start(f32[1,16,1024]{2,1,0:T(8,128)S(1)} %get-tuple-element.89), channel_id=1, source_target_pairs={{16,0},{32,16},{48,32},{64,48},{80,64},{96,80},{112,96},{128,112},... | collective-permute-start | bytes 196616 | tf_op jit(solution)/shard_map/ppermute | solution.py:41
  (17 other events, 99.0 us)
where the time goes:
time: 391 us; the launch traced here: 388 us
  blocking collectives  178 us (46%)
  starting transfers between devices  129 us (33%)
  waiting for transfers between devices  31.6 us (8%)
  local copies, waits for them, and re-layouts  18.5 us (5%)
  other arithmetic  16.4 us (4%)
  between operations  15.5 us (4%)
    psum x20, blocking collectives, one_axis_at_a_time(): return functools.reduce(lax.psum, axes, shard)  178 us
    ppermute x20, starting transfers between devices, with_halo(): lax.ppermute(last, axis, up)  76 us
    ppermute x20, starting transfers between devices, with_halo(): lax.ppermute(initial, axis, [(b, a) for a, b in up])  34.6 us
    ppermute x20, waiting for transfers between devices, with_halo(): lax.ppermute(initial, axis, [(b, a) for a, b in up])  31.5 us
    all_to_all x1, starting transfers between devices, summed_on_arrival(): lax.all_to_all(split_up(shard, dim, devices), axis, 0, 0, tiled=True)  10.9 us
  transfers between devices with their start and end apart: 42, of which 6 were waited for; matrix products, arithmetic and copies ran while one was open for 4% of the time, Pallas kernels for 0%

commit v1 on v0

v1 whole, which is shorter than its diff:
```python
import functools

import jax
import jax.numpy as jnp
from jax import lax
from jax.experimental import pallas as pl
from jax.experimental.pallas import tpu as pltpu
from jax.sharding import PartitionSpec as P

MESH = pl.DeviceIdType.MESH
SUBSTEPS = 4
LANES = 128
EU, EL, EX, EK, EB, EC, EXCHANGES = 0, 4, 7, 8, 9, 13, 15
MERGE = 2
F32 = jnp.float32


def kernel(nx, ny, u_in, dif_in, vel_in, flag_in, x_in, cap_in, k_in, q_in, look_in, u_out, x_out,
           U, HU, SU, L, HL, SL, X, HX, SX, K, HK, SK, B, HB, SB, C, HC, SC,
           CF, W, D, DI, CD, CAP, Q, VEL, DIF, FLAG, LOOK, LKC, GH, FX, DV3, UO, XO,
           TS, TR, PS, PR, AS, AR,
           in_sem, out_sem, xs, xr, ys, yr, ts, tr, ps, pr, a_s, a_r):
    gx, gy = lax.axis_index("gx"), lax.axis_index("gy")
    nr, nc, nz = u_in.shape
    top = nz - LANES
    halves = PS.shape[0]
    per = LANES // nc

    def spot(mx, my):
        return {"device_id": (mx, my), "device_id_type": MESH}

    own = pl.ds(1, nr)
    loads = {}
    for name, src, dst in (
        ("x", x_in, X.at[own]), ("look", look_in, LOOK), ("u", u_in, U.at[0, own]), ("k", k_in, K.at[own]),
        ("flag", flag_in, FLAG), ("dif", dif_in, DIF), ("vel", vel_in, VEL), ("cap", cap_in, CAP), ("q", q_in, Q),
    ):
        loads[name] = pltpu.make_async_copy(src, dst, in_sem.at[len(loads)])
        loads[name].start()

    barrier = pltpu.get_barrier_semaphore()

    def greet_y(d, _):
        pl.semaphore_signal(barrier, inc=1, **spot(gx, lax.rem(gy + d, ny)))
        return 0

    def greet_x(d, _):
        pl.semaphore_signal(barrier, inc=1, **spot(lax.rem(gx + d, nx), gy))
        return 0

    lax.fori_loop(1, ny, greet_y, 0)
    lax.fori_loop(1, nx, greet_x, 0)

    for at_edge, row, side in ((gx == 0, 0, None), (gx == nx - 1, nr + 1, None), (gy == 0, None, 0), (gy == ny - 1, None, 1)):
        @pl.when(at_edge)
        def _(row=row, side=side):
            if side is None:
                for ext in (U, L, B, C):
                    ext[:, row] = jnp.zeros((ext.shape[0], *ext.shape[2:]), F32)
                for ext in (X, K):
                    ext[row] = jnp.zeros(ext.shape[1:], F32)
            else:
                for rim in (HU, HL, HB, HC, HX, HK):
                    rim[:, side] = jnp.zeros((rim.shape[0], *rim.shape[2:]), F32)

    up_x, dn_x, up_y, dn_y = lax.rem(gx + 1, nx), lax.rem(gx + nx - 1, nx), lax.rem(gy + 1, ny), lax.rem(gy + ny - 1, ny)

    def x_pair(ext, e):
        return (
            pltpu.make_async_remote_copy(ext.at[nr], ext.at[0], xs.at[e, 0], xr.at[e, 0], **spot(up_x, gy)),
            pltpu.make_async_remote_copy(ext.at[1], ext.at[nr + 1], xs.at[e, 1], xr.at[e, 1], **spot(dn_x, gy)),
        )

    def y_pair(stage, rim, e):
        return (
            pltpu.make_async_remote_copy(stage.at[1], rim.at[0], ys.at[e, 0], yr.at[e, 0], **spot(gx, up_y)),
            pltpu.make_async_remote_copy(stage.at[0], rim.at[1], ys.at[e, 1], yr.at[e, 1], **spot(gx, dn_y)),
        )

    def start(pair, g, n):
        @pl.when(g < n - 1)
        def _():
            pair[0].start()

        @pl.when(g > 0)
        def _():
            pair[1].start()

    def arrive(pair, g, n):
        @pl.when(g > 0)
        def _():
            pair[0].wait_recv()

        @pl.when(g < n - 1)
        def _():
            pair[1].wait_recv()

    def leave(pair, g, n):
        @pl.when(g < n - 1)
        def _():
            pair[0].wait_send()

        @pl.when(g > 0)
        def _():
            pair[1].wait_send()

    def arrive_both(ext, stage, rim, e):
        arrive(y_pair(stage, rim, e), gy, ny)
        arrive(x_pair(ext, e), gx, nx)

    def leave_both(ext, stage, rim, e):
        leave(y_pair(stage, rim, e), gy, ny)
        leave(x_pair(ext, e), gx, nx)

    links = {}
    for k in range(4):
        links["u", k] = (U.at[k], SU.at[k], HU.at[k], EU + k)
        links["b", k] = (B.at[k], SB.at[k], HB.at[k], EB + k)
    for k in range(3):
        links["l", k] = (L.at[k], SL.at[k], HL.at[k], EL + k)
    for k in range(2):
        links["c", k] = (C.at[k], SC.at[k], HC.at[k], EC + k)
    links["x", 0] = (X, SX.at[0], HX.at[0], EX)
    links["k", 0] = (K, SK.at[0], HK.at[0], EK)

    def rows(body, first=0, count=None, step=1):
        def one(t, _):
            body(first + t * step)
            return 0

        lax.fori_loop(0, nr if count is None else count, one, 0)

    def put(name, i, value):
        ext, stage, _, _ = links[name]
        ext[i + 1] = value
        stage[0, pl.ds(i, 1)] = value[0:1]
        stage[1, pl.ds(i, 1)] = value[nc - 1:nc]

    def produce(name, value_of):
        ext, stage, rim, e = links[name]
        rows(lambda i: put(name, i, value_of(i)), 0, 2, nr - 1)
        start(x_pair(ext, e), gx, nx)
        rows(lambda i: put(name, i, value_of(i)), 1, nr - 2)
        start(y_pair(stage, rim, e), gy, ny)

    def stage_and_send(name):
        ext, stage, rim, e = links[name]
        start(x_pair(ext, e), gx, nx)

        def body(i):
            stage[0, pl.ds(i, 1)] = ext[i + 1, 0:1]
            stage[1, pl.ds(i, 1)] = ext[i + 1, nc - 1:nc]

        rows(body)
        start(y_pair(stage, rim, e), gy, ny)

    def await_halo(name):
        arrive_both(*links[name])

    def around(name, i, low=None):
        ext, _, rim, _ = links[name]
        c = ext[i + 1]
        width = c.shape[1]
        sub = lax.broadcasted_iota(jnp.int32, c.shape, 0)
        lane = lax.broadcasted_iota(jnp.int32, c.shape, 1)
        zero = jnp.zeros_like(c)
        return c, (
            ext[i],
            ext[i + 2],
            jnp.where(sub == 0, rim[0, pl.ds(i, 1)], pltpu.roll(c, 1, 0)),
            jnp.where(sub == nc - 1, rim[1, pl.ds(i, 1)], pltpu.roll(c, nc - 1, 0)),
            jnp.where(lane == 0, zero if low is None else low, pltpu.roll(c, 1, 1)),
            jnp.where(lane == width - 1, zero, pltpu.roll(c, width - 1, 1)),
        )

    def fluid(name, i):
        c, near = around(name, i, GH[i][:, 0:1])
        width = c.shape[1]
        total = CF[6, i, :, 0:width] * c
        for n in range(6):
            total = total + CF[n, i, :, 0:width] * near[n]
        return total

    def scaled_image(name, i):
        c, near = around(name, i)
        lanes = pl.ds(nz - c.shape[1], c.shape[1])
        total = CD[i, :, lanes] * c
        for n in range(6):
            total = total + W[n, i, :, lanes] * (c - near[n])
        return total

    def fluid_coefficients():
        def body(i):
            flag = FLAG[i].astype(F32)
            on = jnp.concatenate([jnp.broadcast_to(flag[:, b:b + 1], (nc, LANES)) for b in range(nz // LANES)], axis=1)
            dif = DIF[i]
            size = 6.0 * dif
            for d in range(3):
                vel = VEL[d, i]
                CF[2 * d, i] = on * (dif + jnp.maximum(vel, 0.0))
                CF[2 * d + 1, i] = on * (dif - jnp.minimum(vel, 0.0))
                size = size + jnp.abs(vel)
            CF[6, i] = 1.0 - on * size

        rows(body)

    def solid_coefficients():
        def body(i):
            c, near = around(("k", 0), i)
            cap = CAP[i]
            total = cap
            faces = [0.5 * (c + v) for v in near]
            for face in faces:
                total = total + face
            inverse = 1.0 / total
            D[i] = total
            DI[i] = inverse
            CD[i] = cap * inverse
            for n in range(6):
                W[n, i] = faces[n] * inverse

        rows(body)

    def first_scaled(i):
        c, near = around(("x", 0), i)
        total = DI[i] * Q[i]
        for n in range(6):
            total = total - W[n, i] * (c - near[n])
        return total

    def send_all(src_of, slots, me, n, peer_of, ssem, rsem):
        def one(d, _):
            peer = lax.rem(me + d, n)
            pltpu.make_async_remote_copy(src_of(peer), slots.at[me], ssem, rsem, **spot(*peer_of(peer))).start()
            return 0

        lax.fori_loop(1, n, one, 0)

    def all_arrived(slots, n, ssem, rsem, peer_of, me):
        most = slots.at[pl.ds(0, n - 1)]
        done = pltpu.make_async_remote_copy(most, most, ssem, rsem, **spot(*peer_of(lax.rem(me + 1, n))))
        done.wait_recv()
        done.wait_send()

    def in_row(p):
        return gx, p

    def in_column(p):
        return p, gy

    sub = lax.broadcasted_iota(jnp.int32, (nc, LANES), 0)
    lane = lax.broadcasted_iota(jnp.int32, (nc, LANES), 1)
    mine = lane == lax.rem(gy, per) * nc + sub

    loads["x"].wait()
    TS[...] = jnp.zeros_like(TS)
    for i in range(nr):
        TS[i:i + 1] = jnp.sum(jnp.where(mine, X[i + 1, :, nz - 1:nz], 0.0), axis=0, keepdims=True)
    TR[gy] = TS[...]
    loads["u"].wait()

    def low_start(i):
        put(("l", 0), i, U[0, i + 1, :, 0:LANES])

    rows(low_start)
    loads["look"].wait()
    look = LOOK[...].astype(F32)
    for i in range(nr):
        here = jnp.broadcast_to(look[i:i + 1], (nc, nc))
        a = lax.broadcasted_iota(jnp.int32, (nc, nc), 0)
        b = lax.broadcasted_iota(jnp.int32, (nc, nc), 1)
        LKC[i] = jnp.broadcast_to(jnp.sum(jnp.where(a == b, here, 0.0), axis=1, keepdims=True), (nc, LANES)).astype(jnp.int32)

    pl.semaphore_wait(barrier, nx + ny - 2)
    send_all(lambda p: TS, TR, gy, ny, in_row, ts, tr)
    ext, stage, rim, e = links["l", 0]
    start(x_pair(ext, e), gx, nx)
    start(y_pair(stage, rim, e), gy, ny)
    loads["k"].wait()
    stage_and_send(("k", 0))
    for name in ("flag", "dif", "vel"):
        loads[name].wait()
    fluid_coefficients()

    all_arrived(TR, ny, ts, tr, in_row, gy)
    for i in range(nr):
        ghost = jnp.zeros((nc, LANES), F32)
        for h in range(halves):
            line = TR[h * per, i:i + 1]
            for s in range(1, min(per, ny)):
                line = line + TR[h * per + s, i:i + 1]
            ghost = ghost + jnp.where(LKC[i] == lane + h * LANES, line, 0.0)
        GH[i] = jnp.broadcast_to(jnp.sum(ghost, axis=1, keepdims=True), (nc, LANES))

    def flux_start(i):
        FX[i] = L[0, i + 1] - GH[i]

    rows(flux_start)
    await_halo(("l", 0))

    def low_step(k):
        def value(i):
            new = fluid(("l", k), i)
            FX[i] = FX[i] + (new - GH[i])
            return new

        return value

    produce(("l", 1), low_step(0))
    stage_and_send(("x", 0))
    await_halo(("l", 1))
    produce(("l", 2), low_step(1))
    stage_and_send(("u", 0))
    loads["cap"].wait()
    loads["q"].wait()
    await_halo(("k", 0))
    solid_coefficients()
    await_halo(("l", 2))
    rows(low_step(2))

    for h in range(halves):
        PS[h] = jnp.zeros(PS.shape[1:], F32)
    for i in range(nr):
        flux = FX[i][:, 0:1] / SUBSTEPS
        for h in range(halves):
            PS[h, i:i + 1] = jnp.sum(jnp.where(LKC[i] == lane + h * LANES, flux, 0.0), axis=0, keepdims=True)
    PR[gy] = PS[gy // per]
    send_all(lambda p: PS.at[p // per], PR, gy, ny, in_row, ps, pr)

    await_halo(("x", 0))
    produce(("b", 0), first_scaled)

    all_arrived(PR, ny, ps, pr, in_row, gy)
    total = PR[0]
    for s in range(1, ny):
        total = total + PR[s]
    GH_lane = lane == LANES - 1
    for i in range(nr):
        came = jnp.sum(jnp.where(mine, total[i:i + 1], 0.0), axis=1, keepdims=True)
        put(("c", 0), i, jnp.where(GH_lane, DI[i, :, top:nz] * came, 0.0))
    ext, stage, rim, e = links["c", 0]
    start(x_pair(ext, e), gx, nx)
    start(y_pair(stage, rim, e), gy, ny)

    await_halo(("u", 0))
    produce(("u", 1), lambda i: fluid(("u", 0), i))

    await_halo(("b", 0))
    produce(("b", 1), lambda i: scaled_image(("b", 0), i))
    await_halo(("c", 0))
    produce(("c", 1), lambda i: scaled_image(("c", 0), i))

    await_halo(("c", 1))

    def top_third(i):
        C[2, i + 1] = C[1, i + 1] - scaled_image(("c", 1), i)

    rows(top_third)

    def third(i):
        value = B[1, i + 1] - scaled_image(("b", 1), i)
        return jnp.concatenate([value[:, 0:top], value[:, top:nz] + C[2, i + 1]], axis=1)

    await_halo(("b", 1))
    produce(("b", 2), third)

    for k in range(MERGE):
        leave_both(*links["b", k])

    def merge(i):
        for k in range(MERGE):
            B[k, i + 1, :, top:nz] = B[k, i + 1, :, top:nz] + C[k, i + 1]

    rows(merge)

    tiles = nz // LANES

    def sums_of(dst, first, count, body):
        def one(t, acc):
            i, b = t // tiles, lax.rem(t, tiles)
            at = pl.ds(pl.multiple_of(b * LANES, LANES), LANES)
            return tuple(a + v for a, v in zip(acc, body(i, at)))

        acc = lax.fori_loop(0, nr * tiles, one, tuple(jnp.zeros((nc, LANES), F32) for _ in range(count)))
        for r, a in enumerate(acc):
            dst[first + r:first + r + 1] = jnp.sum(a, axis=0, keepdims=True)

    def spread_row(use):
        AR[use, 0, gy] = AS[use, 0]
        send_all(lambda p: AS.at[use, 0], AR.at[use, 0], gy, ny, in_row, a_s.at[use, 0], a_r.at[use, 0])

    def spread_column(use):
        all_arrived(AR.at[use, 0], ny, a_s.at[use, 0], a_r.at[use, 0], in_row, gy)
        line = AR[use, 0, 0]
        for s in range(1, ny):
            line = line + AR[use, 0, s]
        AS[use, 1] = line
        AR[use, 1, gx] = line
        send_all(lambda p: AS.at[use, 1], AR.at[use, 1], gx, nx, in_column, a_s.at[use, 1], a_r.at[use, 1])

    def collected(use):
        all_arrived(AR.at[use, 1], nx, a_s.at[use, 1], a_r.at[use, 1], in_column, gx)
        line = AR[use, 1, 0]
        for s in range(1, nx):
            line = line + AR[use, 1, s]
        return jnp.sum(line, axis=1, keepdims=True)

    def two(i, at):
        b0 = B[0, i + 1, :, at]
        weighted = D[i, :, at] * b0
        return weighted * b0, weighted * B[1, i + 1, :, at]

    AS[0, 0] = jnp.zeros(AS.shape[2:], F32)
    sums_of(AS.at[0, 0], 0, 2, two)
    spread_row(0)

    await_halo(("u", 1))
    produce(("u", 2), lambda i: fluid(("u", 1), i))

    spread_column(0)
    await_halo(("b", 2))
    produce(("b", 3), lambda i: 2.0 * (B[2, i + 1] - scaled_image(("b", 2), i)) - B[1, i + 1])

    pair = collected(0)
    rho = pair[1:2] / pair[0:1]

    def thirteen(i, at):
        c0, c1, c2, c3 = (B[k, i + 1, :, at] for k in range(4))
        m1 = c1 - c2
        m2 = c2 - 0.5 * (c3 + c1)
        v1 = c1 - rho * c0
        v2 = c2 - rho * (c0 - c1)
        v3 = c3 - rho * (c0 - 2.0 * (c1 + c2))
        weight = D[i, :, at]
        w0, w1, w2, w3 = (weight * v for v in (c0, v1, v2, v3))
        DV3[i, :, at] = w3
        n1 = m1 - rho * c1
        n2 = m2 - rho * c2
        n3 = rho * (c1 - 2.0 * (m1 + m2))
        return (
            w0 * c0, w1 * c0, w2 * c0, w3 * c0,
            w0 * c1, w1 * c1, w2 * c1, w3 * c1,
            w1 * n1, w2 * n1, w3 * n1,
            w2 * n2, w3 * n2,
            -(w3 * n3),
        )

    AS[1, 0] = jnp.zeros(AS.shape[2:], F32)
    sums_of(AS.at[1, 0], 0, 14, thirteen)

    await_halo(("u", 2))
    produce(("u", 3), lambda i: fluid(("u", 2), i))

    await_halo(("b", 3))

    def last(i, acc):
        value = DV3[i] * scaled_image(("b", 3), i)
        for b in range(tiles):
            acc = acc + value[:, b * LANES:(b + 1) * LANES]
        return acc

    AS[1, 0, 14:15] = jnp.sum(lax.fori_loop(0, nr, last, jnp.zeros((nc, LANES), F32)), axis=0, keepdims=True)
    spread_row(1)

    await_halo(("u", 3))
    rows(lambda i: UO.__setitem__(i, fluid(("u", 3), i)))
    u_done = pltpu.make_async_copy(UO, u_out, out_sem.at[0])
    u_done.start()

    spread_column(1)
    col = collected(1)
    e = [col[r:r + 1] for r in range(15)]
    g = e[0:4]
    H = {(0, 0): e[4], (1, 0): e[5], (2, 0): e[6], (3, 0): e[7], (1, 1): e[8], (2, 1): e[9], (3, 1): e[10],
         (2, 2): e[11], (3, 2): e[12], (3, 3): e[13] + e[14]}
    inv, low = {}, {}
    for j in range(4):
        pivot = H[j, j]
        for m in range(j):
            pivot = pivot - low[j, m] * H[j, m]
        inv[j] = jnp.where(pivot > 0.0, 1.0 / pivot, 0.0)
        for i in range(j + 1, 4):
            value = H[i, j]
            for m in range(j):
                value = value - low[j, m] * H[i, m]
            H[i, j] = value
            low[i, j] = value * inv[j]
    y = list(g)
    for i in range(4):
        for m in range(i):
            y[i] = y[i] - low[i, m] * y[m]
    y = [y[i] * inv[i] for i in range(4)]
    for i in range(3, -1, -1):
        for m in range(i + 1, 4):
            y[i] = y[i] - low[m, i] * y[m]
    f0 = y[0] - rho * (y[1] + y[2] + y[3])
    f1 = y[1] + rho * (y[2] + 2.0 * y[3])
    f2 = y[2] + 2.0 * rho * y[3]

    def finish(i):
        XO[i] = X[i + 1] + ((f0 * B[0, i + 1] + f1 * B[1, i + 1]) + (f2 * B[2, i + 1] + y[3] * B[3, i + 1]))

    rows(finish)
    x_done = pltpu.make_async_copy(XO, x_out, out_sem.at[1])
    x_done.start()

    for name, link in links.items():
        if name not in (("b", 0), ("b", 1)):
            leave_both(*link)
    u_done.wait()
    x_done.wait()


def solution(mesh):
    nx, ny = mesh.shape["gx"], mesh.shape["gy"]

    def local(u, dif, vel, flag, x, cap, k, q, look):
        nr, nc, nz = u.shape
        halves = max(1, nc * ny // LANES)
        most = max(nx, ny)
        vm = lambda *shape: pltpu.VMEM(shape, F32)
        dma = lambda *shape: pltpu.SemaphoreType.DMA(shape)

        def linked(count, width):
            return [vm(count, nr + 2, nc, width), vm(count, 2, nr, width), vm(count, 2, nr, width)]

        def linked_one(width):
            return [vm(nr + 2, nc, width), vm(1, 2, nr, width), vm(1, 2, nr, width)]

        block = (nr, nc, nz)
        scratch = [
            *linked(4, nz), *linked(3, LANES), *linked_one(nz), *linked_one(nz), *linked(4, nz), *linked(3, LANES),
            vm(7, *block), vm(6, *block), vm(*block), vm(*block), vm(*block), vm(*block), vm(*block),
            vm(3, *block), vm(*block), pltpu.VMEM(flag.shape, jnp.int32), pltpu.VMEM(look.shape, jnp.int32),
            pltpu.VMEM((nr, nc, LANES), jnp.int32), vm(nr, nc, LANES), vm(nr, nc, LANES), vm(*block), vm(*block), vm(*block),
            vm(8, LANES), vm(ny, 8, LANES), vm(halves, 8, LANES), vm(ny, 8, LANES),
            vm(2, 2, 16, LANES), vm(2, 2, most, 16, LANES),
            dma(9), dma(2), dma(EXCHANGES, 2), dma(EXCHANGES, 2), dma(EXCHANGES, 2), dma(EXCHANGES, 2),
            dma(), dma(), dma(), dma(), dma(2, 2), dma(2, 2),
        ]
        any_space = pl.BlockSpec(memory_space=pl.ANY)
        return pl.pallas_call(
            functools.partial(kernel, nx, ny),
            out_shape=(jax.ShapeDtypeStruct(block, F32), jax.ShapeDtypeStruct(block, F32)),
            in_specs=[any_space] * 9,
            out_specs=(any_space, any_space),
            scratch_shapes=scratch,
            compiler_params=pltpu.CompilerParams(collective_id=0, has_side_effects=True, vmem_limit_bytes=40 * 1024 * 1024),
            name="window",
        )(u, dif, vel, flag, x, cap, k, q, look)

    spec = P("gx", "gy", None)
    return jax.shard_map(
        local,
        mesh=mesh,
        in_specs=(spec, spec, P(None, "gx", "gy", None), spec, spec, spec, spec, spec, P("gx", "gy")),
        out_specs=(spec, spec),
        check_vma=False,
    )
```

time: 391 us -> 83.5 us (0.21)
  blocking collectives: 178 us -> 0 us
  starting transfers between devices: 129 us -> 0 us
  Pallas kernels: 0 us -> 73.4 us
  waiting for transfers between devices: 31.6 us -> 0 us
  other arithmetic: 16.4 us -> 0 us
  between operations: 15.5 us -> 0.65 us
  local copies, waits for them, and re-layouts: 18.5 us -> 9.04 us
    psum x20 -> x0, blocking collectives: 178 us -> none  [one_axis_at_a_time(): return functools.reduce(lax.psum, axes, shard)]
    ppermute x40 -> x0, starting transfers between devices: 111 us -> none  [the longest x20 76 us: with_halo(): lax.ppermute(last, axis, up)]
    pallas_call x0 -> x1, Pallas kernels: none -> 73.4 us  [local(): pl.pallas_call(functools.partial(kernel, nx, ny), out_shape=(jax.ShapeDty...]
    ppermute x40 -> x0, waiting for transfers between devices: 31.6 us -> none  [the longest x20 31.5 us: with_halo(): lax.ppermute(initial, axis, [(b, a) for a, b in up])]
    all_to_all x2 -> x0, starting transfers between devices: 18.1 us -> none  [the longest x1 10.9 us: summed_on_arrival(): lax.all_to_all(split_up(shard, dim, devices), axis, 0, 0, tiled=True)]
    slice x45 -> x0, local copies, waits for them, and re-layouts: 9.6 us -> none  [the longest x25 4.43 us: with_halo(): last = lax.slice_in_dim(shard, length - width, length, axis=dim)]
    reduce_sum x8 -> x0, other arithmetic: 7.41 us -> none  [the longest x4 5.29 us: paired(): jnp.sum(scaled_now * image_now)]
    unnamed x57 -> x19, local copies, waits for them, and re-layouts: 3.11 us -> 9.04 us
  transfers between devices with their start and end apart: 42 -> 0, of which waited for: 6 -> 0; matrix products, arithmetic and copies ran while one was open for 4% -> 0% of each run, Pallas kernels for 0% -> 0%
where the time goes in v1:
time: 83.5 us; the launch traced here: 83.1 us
  Pallas kernels  73.4 us (88%)
  local copies, waits for them, and re-layouts  9.04 us (11%)
    pallas_call x1, Pallas kernels, local(): pl.pallas_call(functools.partial(kernel, nx, ny), out_shape=(jax.ShapeDty...  73.4 us
    unnamed x19, local copies, waits for them, and re-layouts  9.04 us

profile of v1, /device:TPU:1, one launch (start us, length us, event | category | flops | bytes accessed | tf_op | source)
XLA Modules:
  0.0 83.1 jit_solution(13790443734508963408)
XLA Ops:
  0.6 0.0 copy-start.7
  0.6 0.8 copy.11.flag_in
  1.4 0.0 copy-done.7
  1.4 0.0 copy-start
  1.4 1.1 %copy-done = f32[3,4,16,1024]{3,2,1,0:T(8,128)S(1)} copy-done((f32[3,4,16,1024]{3,2,1,0:T(8,128)S(1)}, f32[3,4,16,1024]{3,2,1,0:T(8,128)}, u32[]{:S(2)}) %copy-start) | copy-done | bytes 786456
  2.6 0.0 copy-start.1
  2.6 0.9 %copy-done.1 = f32[4,16,1024]{2,1,0:T(8,128)S(1)} copy-done((f32[4,16,1024]{2,1,0:T(8,128)S(1)}, f32[4,16,1024]{2,1,0:T(8,128)}, u32[]{:S(2)}) %copy-start.1) | copy-done | bytes 262168
  3.5 0.0 copy-start.2
  3.5 0.9 %copy-done.2 = f32[4,16,1024]{2,1,0:T(8,128)S(1)} copy-done((f32[4,16,1024]{2,1,0:T(8,128)S(1)}, f32[4,16,1024]{2,1,0:T(8,128)}, u32[]{:S(2)}) %copy-start.2) | copy-done | bytes 262168
  4.5 0.0 copy-start.3
  4.5 0.9 %copy-done.3 = f32[4,16,1024]{2,1,0:T(8,128)S(1)} copy-done((f32[4,16,1024]{2,1,0:T(8,128)S(1)}, f32[4,16,1024]{2,1,0:T(8,128)}, u32[]{:S(2)}) %copy-start.3) | copy-done | bytes 262168
  5.4 0.0 copy-start.4
  5.4 0.9 %copy-done.4 = f32[4,16,1024]{2,1,0:T(8,128)S(1)} copy-done((f32[4,16,1024]{2,1,0:T(8,128)S(1)}, f32[4,16,1024]{2,1,0:T(8,128)}, u32[]{:S(2)}) %copy-start.4) | copy-done | bytes 262168
  6.4 0.0 copy-start.5
  6.4 0.9 %copy-done.5 = f32[4,16,1024]{2,1,0:T(8,128)S(1)} copy-done((f32[4,16,1024]{2,1,0:T(8,128)S(1)}, f32[4,16,1024]{2,1,0:T(8,128)}, u32[]{:S(2)}) %copy-start.5) | copy-done | bytes 262168
  7.3 0.0 copy-start.6
  7.3 0.9 %copy-done.6 = f32[4,16,1024]{2,1,0:T(8,128)S(1)} copy-done((f32[4,16,1024]{2,1,0:T(8,128)S(1)}, f32[4,16,1024]{2,1,0:T(8,128)}, u32[]{:S(2)}) %copy-start.6) | copy-done | bytes 262168
  8.3 73.4 %window.1 = (f32[4,16,1024]{2,1,0:T(8,128)S(1)}, f32[4,16,1024]{2,1,0:T(8,128)S(1)}) custom-call(f32[4,16,1024]{2,1,0:T(8,128)S(1)} %copy-done.1, f32[4,16,1024]{2,1,0:T(8,128)S(1)} %copy-done.2, f32[3,4,16,1024]{3,2,1,0:T(8,128)S(1)} %copy-done, s32[4,16,8]{2,1,0:T(8,128)S(1)} %copy.11.flag_in, f32[4,16,1024]{2,1,0:T(8,128)S(1)} %copy-done.3, ...), custom_call_target="tpu_custom_call" | custom-call | tf_op jit(solution)/shard_map/window/pallas_call | solution.py:542
  81.7 0.7 copy.14
  82.4 0.7 copy.15
Async XLA Ops:
  0.6 0.8 copy-start.7
  1.4 1.1 %copy-start = (f32[3,4,16,1024]{3,2,1,0:T(8,128)S(1)}, f32[3,4,16,1024]{3,2,1,0:T(8,128)}, u32[]{:S(2)}) copy-start(f32[3,4,16,1024]{3,2,1,0:T(8,128)} %vel_in.1) | copy-start | bytes 2359300
  2.6 0.9 %copy-start.1 = (f32[4,16,1024]{2,1,0:T(8,128)S(1)}, f32[4,16,1024]{2,1,0:T(8,128)}, u32[]{:S(2)}) copy-start(f32[4,16,1024]{2,1,0:T(8,128)} %u_in.1) | copy-start | bytes 786436
  3.5 0.9 %copy-start.2 = (f32[4,16,1024]{2,1,0:T(8,128)S(1)}, f32[4,16,1024]{2,1,0:T(8,128)}, u32[]{:S(2)}) copy-start(f32[4,16,1024]{2,1,0:T(8,128)} %dif_in.1) | copy-start | bytes 786436
  4.5 0.9 %copy-start.3 = (f32[4,16,1024]{2,1,0:T(8,128)S(1)}, f32[4,16,1024]{2,1,0:T(8,128)}, u32[]{:S(2)}) copy-start(f32[4,16,1024]{2,1,0:T(8,128)} %x_in.1) | copy-start | bytes 786436
  5.4 0.9 %copy-start.4 = (f32[4,16,1024]{2,1,0:T(8,128)S(1)}, f32[4,16,1024]{2,1,0:T(8,128)}, u32[]{:S(2)}) copy-start(f32[4,16,1024]{2,1,0:T(8,128)} %cap_in.1) | copy-start | bytes 786436
  6.4 0.9 %copy-start.5 = (f32[4,16,1024]{2,1,0:T(8,128)S(1)}, f32[4,16,1024]{2,1,0:T(8,128)}, u32[]{:S(2)}) copy-start(f32[4,16,1024]{2,1,0:T(8,128)} %k_in.1) | copy-start | bytes 786436
  7.3 0.9 %copy-start.6 = (f32[4,16,1024]{2,1,0:T(8,128)S(1)}, f32[4,16,1024]{2,1,0:T(8,128)}, u32[]{:S(2)}) copy-start(f32[4,16,1024]{2,1,0:T(8,128)} %q_in.1) | copy-start | bytes 786436

commit v2 on v1

v2 whole, which is shorter than its diff:
```python
import functools

import jax
import jax.numpy as jnp
from jax import lax
from jax.experimental import pallas as pl
from jax.experimental.pallas import tpu as pltpu
from jax.sharding import PartitionSpec as P

MESH = pl.DeviceIdType.MESH
SUBSTEPS = 4
LANES = 128
X_U, X_L, X_X, X_K, X_B, X_C, EXCHANGES = 0, 4, 7, 8, 9, 13, 14
ORDER = (
    "T", "L0", "K", "X", "LK", "CF", "G", "L1", "E", "W", "L2", "B0", "L3", "EW", "U0", "B1", "C", "R1", "B2", "U1",
    "R2", "B3", "R3", "U2", "H", "U3", "A2", "U4", "A3",
)
F32 = jnp.float32


def kernel(nx, ny, u_in, dif_in, vel_in, flag_in, x_in, cap_in, k_in, q_in, look_in, u_out, x_out,
           U, HU, SU, L, HL, SL, X, HX, SX, K, HK, SK, B, HB, SB, C, HC, SC,
           CF, W, D, DI, CD, CAP, Q, VEL, DIF, FLAG, LOOK, LKC, GH, FX, DV3,
           EP, EK, EC, WE, CE, TS, TR, PS, PR, AW, AS, AR,
           in_sem, xs, xr, ys, yr, ts, tr, es, er, ps, pr, a_s, a_r):
    gx, gy = lax.axis_index("gx"), lax.axis_index("gy")
    nr, nc, nz = u_in.shape
    top = nz - LANES
    tiles = nz // LANES
    halves = max(1, nc * ny // LANES)
    per = LANES // nc
    waiting, leaving = {}, {}

    def spot(mx, my):
        return {"device_id": (mx, my), "device_id_type": MESH}

    own = pl.ds(1, nr)
    loads = {}
    for name, src, dst in (
        ("x", x_in, X.at[own]), ("look", look_in, LOOK), ("u", u_in, U.at[0, own]), ("k", k_in, K.at[own]),
        ("flag", flag_in, FLAG), ("dif", dif_in, DIF), ("vel", vel_in, VEL), ("cap", cap_in, CAP), ("q", q_in, Q),
    ):
        loads[name] = pltpu.make_async_copy(src, dst, in_sem.at[len(loads)])
        loads[name].start()

    def loaded(*names):
        for name in names:
            if name in loads:
                loads.pop(name).wait()

    EP[...] = jnp.zeros_like(EP)
    barrier = pltpu.get_barrier_semaphore()

    def greet_y(d, _):
        pl.semaphore_signal(barrier, inc=1, **spot(gx, lax.rem(gy + d, ny)))
        return 0

    def greet_x(d, _):
        pl.semaphore_signal(barrier, inc=1, **spot(lax.rem(gx + d, nx), gy))
        return 0

    def greet_beside(mx):
        def one(d, _):
            pl.semaphore_signal(barrier, inc=1, **spot(mx, lax.rem(gy + d, ny)))
            return 0

        lax.fori_loop(1, ny, one, 0)

    lax.fori_loop(1, ny, greet_y, 0)
    lax.fori_loop(1, nx, greet_x, 0)
    beside = ((gx > 0, lax.rem(gx + nx - 1, nx)), (gx < nx - 1, lax.rem(gx + 1, nx)))
    for there, mx in beside:
        @pl.when(there)
        def _(mx=mx):
            greet_beside(mx)

    def all_here():
        rows_beside = jnp.where(gx > 0, 1, 0) + jnp.where(gx < nx - 1, 1, 0)
        pl.semaphore_wait(barrier, nx + ny - 2 + rows_beside * (ny - 1))

    for at_edge, row, side in ((gx == 0, 0, None), (gx == nx - 1, nr + 1, None), (gy == 0, None, 0), (gy == ny - 1, None, 1)):
        @pl.when(at_edge)
        def _(row=row, side=side):
            if side is None:
                for ext in (U, L, B, C):
                    ext[:, row] = jnp.zeros((ext.shape[0], *ext.shape[2:]), F32)
                for ext in (X, K):
                    ext[row] = jnp.zeros(ext.shape[1:], F32)
            else:
                for rim in (HU, HL, HB, HC, HX, HK):
                    rim[:, side] = jnp.zeros((rim.shape[0], *rim.shape[2:]), F32)

    up_x, dn_x, up_y, dn_y = lax.rem(gx + 1, nx), lax.rem(gx + nx - 1, nx), lax.rem(gy + 1, ny), lax.rem(gy + ny - 1, ny)

    def x_pair(ext, e):
        return (
            pltpu.make_async_remote_copy(ext.at[nr], ext.at[0], xs.at[e, 0], xr.at[e, 0], **spot(up_x, gy)),
            pltpu.make_async_remote_copy(ext.at[1], ext.at[nr + 1], xs.at[e, 1], xr.at[e, 1], **spot(dn_x, gy)),
        )

    def y_pair(stage, rim, e):
        return (
            pltpu.make_async_remote_copy(stage.at[1], rim.at[0], ys.at[e, 0], yr.at[e, 0], **spot(gx, up_y)),
            pltpu.make_async_remote_copy(stage.at[0], rim.at[1], ys.at[e, 1], yr.at[e, 1], **spot(gx, dn_y)),
        )

    def start(pair, g, n):
        @pl.when(g < n - 1)
        def _():
            pair[0].start()

        @pl.when(g > 0)
        def _():
            pair[1].start()

    def arrive(pair, g, n):
        @pl.when(g > 0)
        def _():
            pair[0].wait_recv()

        @pl.when(g < n - 1)
        def _():
            pair[1].wait_recv()

    def leave(pair, g, n):
        @pl.when(g < n - 1)
        def _():
            pair[0].wait_send()

        @pl.when(g > 0)
        def _():
            pair[1].wait_send()

    links = {}
    for k in range(4):
        links["u", k] = (U.at[k], SU.at[k], HU.at[k], X_U + k)
        links["b", k] = (B.at[k], SB.at[k], HB.at[k], X_B + k)
    for k in range(3):
        links["l", k] = (L.at[k], SL.at[k], HL.at[k], X_L + k)
    links["c", 3] = (C.at[0], SC.at[0], HC.at[0], X_C)
    links["x", 0] = (X, SX.at[0], HX.at[0], X_X)
    links["k", 0] = (K, SK.at[0], HK.at[0], X_K)

    def send_x(name):
        ext, _, _, e = links[name]
        start(x_pair(ext, e), gx, nx)

    def send_y(name):
        ext, stage, rim, e = links[name]
        start(y_pair(stage, rim, e), gy, ny)

        def came():
            arrive(y_pair(stage, rim, e), gy, ny)
            arrive(x_pair(ext, e), gx, nx)

        def left():
            leave(y_pair(stage, rim, e), gy, ny)
            leave(x_pair(ext, e), gx, nx)

        waiting[name], leaving[name] = came, left

    def await_halo(*names):
        for name in names:
            if name in waiting:
                waiting.pop(name)()

    def rows(body, first=0, count=None, step=1):
        def one(t, _):
            body(first + t * step)
            return 0

        lax.fori_loop(0, nr if count is None else count, one, 0)

    def put(name, i, value):
        ext, stage, _, _ = links[name]
        ext[i + 1] = value
        stage[0, pl.ds(i, 1)] = value[0:1]
        stage[1, pl.ds(i, 1)] = value[nc - 1:nc]

    def produce(name, value_of):
        rows(lambda i: put(name, i, value_of(i)), 0, 2, nr - 1)
        send_x(name)
        rows(lambda i: put(name, i, value_of(i)), 1, nr - 2)
        send_y(name)

    def stage_and_send(name):
        ext, stage, _, _ = links[name]
        send_x(name)

        def body(i):
            stage[0, pl.ds(i, 1)] = ext[i + 1, 0:1]
            stage[1, pl.ds(i, 1)] = ext[i + 1, nc - 1:nc]

        rows(body)
        send_y(name)

    def around(name, i, low=None):
        ext, _, rim, _ = links[name]
        c = ext[i + 1]
        width = c.shape[1]
        sub = lax.broadcasted_iota(jnp.int32, c.shape, 0)
        lane = lax.broadcasted_iota(jnp.int32, c.shape, 1)
        zero = jnp.zeros_like(c)
        return c, (
            ext[i],
            ext[i + 2],
            jnp.where(sub == 0, rim[0, pl.ds(i, 1)], pltpu.roll(c, 1, 0)),
            jnp.where(sub == nc - 1, rim[1, pl.ds(i, 1)], pltpu.roll(c, nc - 1, 0)),
            jnp.where(lane == 0, zero if low is None else low, pltpu.roll(c, 1, 1)),
            jnp.where(lane == width - 1, zero, pltpu.roll(c, width - 1, 1)),
        )

    def fluid(name, i):
        c, near = around(name, i, GH[i][:, 0:1])
        width = c.shape[1]
        total = CF[6, i, :, 0:width] * c
        for n in range(6):
            total = total + CF[n, i, :, 0:width] * near[n]
        return total

    def scaled_image(name, i):
        c, near = around(name, i)
        lanes = pl.ds(nz - c.shape[1], c.shape[1])
        total = CD[i, :, lanes] * c
        for n in range(6):
            total = total + W[n, i, :, lanes] * (c - near[n])
        return total

    def fluid_coefficients():
        square = (nc, nc)
        diagonal = lax.broadcasted_iota(jnp.int32, square, 0) == lax.broadcasted_iota(jnp.int32, square, 1)

        def body(i):
            flag = FLAG[i].astype(F32)
            blocks = []
            for b in range(tiles):
                column = jnp.sum(jnp.where(diagonal, jnp.broadcast_to(flag[b:b + 1], square), 0.0), axis=1, keepdims=True)
                blocks.append(jnp.broadcast_to(column, (nc, LANES)))
            on = jnp.concatenate(blocks, axis=1)
            dif = DIF[i]
            size = 6.0 * dif
            for d in range(3):
                vel = VEL[d, i]
                CF[2 * d, i] = on * (dif + jnp.maximum(vel, 0.0))
                CF[2 * d + 1, i] = on * (dif - jnp.minimum(vel, 0.0))
                size = size + jnp.abs(vel)
            CF[6, i] = 1.0 - on * size

        rows(body)

    def solid_coefficients():
        def body(i):
            c, near = around(("k", 0), i)
            cap = CAP[i]
            total = cap
            faces = [0.5 * (c + v) for v in near]
            for face in faces:
                total = total + face
            inverse = 1.0 / total
            D[i] = total
            DI[i] = inverse
            CD[i] = cap * inverse
            for n in range(6):
                W[n, i] = faces[n] * inverse

        rows(body)

    def first_scaled(i):
        c, near = around(("x", 0), i)
        total = DI[i] * Q[i]
        for n in range(6):
            total = total - W[n, i] * (c - near[n])
        return total

    def in_row(p):
        return gx, p

    def in_column(p):
        return p, gy

    def send_all(name, src_of, slots, me, n, peer_of, ssem, rsem):
        def one(d, _):
            peer = lax.rem(me + d, n)
            pltpu.make_async_remote_copy(src_of(peer), slots.at[me], ssem, rsem, **spot(*peer_of(peer))).start()
            return 0

        lax.fori_loop(1, n, one, 0)
        most = slots.at[pl.ds(0, n - 1)]
        done = pltpu.make_async_remote_copy(most, most, ssem, rsem, **spot(*peer_of(lax.rem(me + 1, n))))
        waiting[name], leaving[name] = done.wait_recv, done.wait_send

    sub = lax.broadcasted_iota(jnp.int32, (nc, LANES), 0)
    lane = lax.broadcasted_iota(jnp.int32, (nc, LANES), 1)
    mine = lane == lax.rem(gy, per) * nc + sub
    equal = lane == sub

    def collect_top():
        loaded("x", "look")
        for i in range(nr):
            TS[i:i + 1] = jnp.sum(jnp.where(mine, X[i + 1, :, nz - 1:nz], 0.0), axis=0, keepdims=True)
        TR[gy] = TS[...]
        all_here()
        send_all("t", lambda p: TS, TR, gy, ny, in_row, ts, tr)

    def low_start():
        loaded("u")
        rows(lambda i: put(("l", 0), i, U[0, i + 1, :, 0:LANES]))
        send_x(("l", 0))
        send_y(("l", 0))

    def partners():
        look = LOOK[...].astype(F32)
        square = (nc, nc)
        diagonal = lax.broadcasted_iota(jnp.int32, square, 0) == lax.broadcasted_iota(jnp.int32, square, 1)
        for i in range(nr):
            here = jnp.broadcast_to(look[i:i + 1], square)
            column = jnp.sum(jnp.where(diagonal, here, 0.0), axis=1, keepdims=True)
            LKC[i] = jnp.broadcast_to(column, (nc, LANES)).astype(jnp.int32)
        goal = jnp.full((nc, LANES), -1.0, F32)
        for i in range(nr):
            goal = jnp.where(lane == i * nc + sub, LKC[i].astype(F32), goal)
        PS[1:2] = jnp.max(goal, axis=0, keepdims=True)

    def ghosts():
        await_halo("t")
        for i in range(nr):
            ghost = jnp.zeros((nc, LANES), F32)
            for h in range(halves):
                line = TR[h * per, i:i + 1]
                for s in range(1, min(per, ny)):
                    line = line + TR[h * per + s, i:i + 1]
                ghost = ghost + jnp.where(LKC[i] == lane + h * LANES, line, 0.0)
            GH[i] = jnp.broadcast_to(jnp.sum(ghost, axis=1, keepdims=True), (nc, LANES))
            FX[i] = L[0, i + 1] - GH[i]

    def low_step(k):
        def value(i):
            new = fluid(("l", k), i)
            FX[i] = FX[i] + (new - GH[i])
            return new

        return value

    wide = (EP.shape[1], LANES)
    pad = (wide[0] - nc) // 2
    wide_sub = lax.broadcasted_iota(jnp.int32, wide, 0)
    wide_lane = lax.broadcasted_iota(jnp.int32, wide, 1)
    keep = LANES // 16

    def flux_home():
        await_halo(("l", 2))
        rows(low_step(2))
        value = jnp.zeros((nc, LANES), F32)
        for i in range(nr):
            value = jnp.where(lane == i * nc + sub, FX[i][:, 0:1] / SUBSTEPS, value)
        PS[0:1] = jnp.sum(value, axis=0, keepdims=True)
        PR[1, gy] = PS[...]
        send_all("p", lambda p: PS, PR.at[1], gy, ny, in_row, ps.at[1], pr.at[1])
        for there, mx, group in ((gx < nx - 1, lax.rem(gx + 1, nx), 0), (gx > 0, lax.rem(gx + nx - 1, nx), 2)):
            @pl.when(there)
            def _(mx=mx, group=group):
                def one(d, _):
                    peer = lax.rem(gy + d, ny)
                    pltpu.make_async_remote_copy(PS, PR.at[group, gy], ps.at[group], pr.at[group], **spot(mx, peer)).start()
                    return 0

                lax.fori_loop(0, ny, one, 0)

        def whole(group):
            return pltpu.make_async_remote_copy(PR.at[group], PR.at[group], ps.at[group], pr.at[group], **spot(up_x, gy))

        def came():
            for there, group in ((gx > 0, 0), (gx < nx - 1, 2)):
                @pl.when(there)
                def _(group=group):
                    whole(group).wait_recv()

        def left():
            for there, group in ((gx < nx - 1, 0), (gx > 0, 2)):
                @pl.when(there)
                def _(group=group):
                    whole(group).wait_send()

        waiting["p2"], leaving["p2"] = came, left

    def edge_copies():
        loaded("k", "cap")
        total = jnp.zeros((nc, LANES), F32)
        for i in range(nr):
            at = i * 2 * keep
            total = jnp.where((lane >= at) & (lane < at + keep), pltpu.roll(K[i + 1, :, top:nz], at + keep, 1), total)
            total = jnp.where((lane >= at + keep) & (lane < at + 2 * keep), pltpu.roll(CAP[i, :, top:nz], (at + 2 * keep) % LANES, 1), total)
        EP[1, pad:pad + nc] = total
        pairs = []
        for dx in (-1, 0, 1):
            for dy in (-1, 0, 1):
                if dx or dy:
                    src = {0: pl.ds(pad, nc), 1: pl.ds(nc, pad), -1: pl.ds(pad, pad)}[dy]
                    dst = {0: pl.ds(pad, nc), 1: pl.ds(0, pad), -1: pl.ds(pad + nc, pad)}[dy]
                    target = (gx + dx >= 0) & (gx + dx < nx) & (gy + dy >= 0) & (gy + dy < ny)
                    source = (gx - dx >= 0) & (gx - dx < nx) & (gy - dy >= 0) & (gy - dy < ny)
                    to = spot(lax.rem(gx + dx + nx, nx), lax.rem(gy + dy + ny, ny))
                    n = len(pairs)
                    pairs.append((target, source, pltpu.make_async_remote_copy(EP.at[1, src], EP.at[1 - dx, dst], es.at[n], er.at[n], **to)))
        for target, _, copy in pairs:
            pl.when(target)(copy.start)

        def came():
            for _, source, copy in pairs:
                pl.when(source)(copy.wait_recv)

        def left():
            for target, _, copy in pairs:
                pl.when(target)(copy.wait_send)

        waiting["e"], leaving["e"] = came, left

    def wide_around(ref, x, count):
        c = ref[x:x + count]
        return c, (ref[x - 1:x - 1 + count], ref[x + 1:x + 1 + count], pltpu.roll(c, 1, 1), pltpu.roll(c, wide[0] - 1, 1),
                   pltpu.roll(c, 1, 2), pltpu.roll(c, LANES - 1, 2))

    def edge_coefficients():
        await_halo("e")
        for x in range(3 * nr):
            at = x % nr * 2 * keep
            packed_row = EP[x // nr]
            EK[x] = jnp.where(wide_lane >= LANES - keep, pltpu.roll(packed_row, LANES - keep - at, 1), 0.0)
            EC[x] = pltpu.roll(packed_row, LANES - 2 * keep - at, 1)

        x, count = 1, 3 * nr - 2
        block = (count, *wide)
        c, near = wide_around(EK, x, count)
        at_row = lax.broadcasted_iota(jnp.int32, block, 0) + (gx * nr - nr + x)
        across = lax.broadcasted_iota(jnp.int32, block, 1) + (gy * nc - pad)
        along = lax.broadcasted_iota(jnp.int32, block, 2)
        inside = (across >= 0) & (across < ny * nc) & (along >= LANES - keep) & (at_row >= 0) & (at_row < nx * nr)
        near = near[:5] + (jnp.where(along == LANES - 1, 0.0, near[5]),)
        faces = [0.5 * (c + v) for v in near]
        cap = EC[x:x + count]
        total = cap
        for face in faces:
            total = total + face
        inverse = jnp.where(inside, 1.0 / jnp.where(inside, total, 1.0), 0.0)
        for n in range(6):
            WE[n, x:x + count] = faces[n] * inverse
        WE[6, x:x + count] = jnp.where(inside, cap, 0.0) * inverse
        WE[7, x:x + count] = inverse

    def flux_arrives():
        await_halo("p", "p2")
        column = (wide_sub + (gy * nc - pad)).astype(F32)
        for group in range(3):
            parts = []
            for first in range(0, ny, 4):
                total = jnp.zeros(wide, F32)
                for s in range(first, min(first + 4, ny)):
                    total = jnp.where(PR[group, s, 1:2] == column, PR[group, s, 0:1], total)
                parts.append(total)
            total = functools.reduce(jnp.add, parts)
            there = {0: gx > 0, 1: gx >= 0, 2: gx < nx - 1}[group]
            for i in range(nr):
                x = group * nr + i
                came = jnp.sum(jnp.where((wide_lane >= i * nc) & (wide_lane < (i + 1) * nc), total, 0.0), axis=1, keepdims=True)
                CE[0, x] = jnp.where((wide_lane == LANES - 1) & there, WE[7, x] * came, 0.0)
        for k in range(1, 4):
            x, count = 1 + k, 3 * nr - 2 - 2 * k
            c, near = wide_around(CE.at[k - 1], x, count)
            total = WE[6, x:x + count] * c
            for n in range(6):
                total = total + WE[n, x:x + count] * (c - near[n])
            if k > 1:
                total = c - total
            if k > 2:
                total = 2.0 * total - CE[k - 2, x:x + count]
            CE[k, x:x + count] = total
        rows(lambda i: put(("c", 3), i, CE[3, nr + i, pad:pad + nc]))
        send_x(("c", 3))
        send_y(("c", 3))

    def field(k):
        def value(i):
            if k == 1:
                return scaled_image(("b", 0), i)
            last = B[k - 1, i + 1] - scaled_image(("b", k - 1), i)
            return last if k == 2 else 2.0 * last - B[k - 2, i + 1]

        await_halo(("b", k - 1))
        produce(("b", k), value)

    def packed(use, count):
        column = jnp.sum(AW[use], axis=1, keepdims=True)
        return jnp.sum(jnp.where(equal, column, 0.0), axis=0, keepdims=True)

    def added(slots, n):
        line = slots[0]
        for s in range(1, n):
            line = line + slots[s]
        return line

    def spread_row(use):
        line = packed(use, 0)
        AS[use, 0] = line
        AR[use, 0, gy] = line
        send_all(("row", use), lambda p: AS.at[use, 0], AR.at[use, 0], gy, ny, in_row, a_s.at[use, 0], a_r.at[use, 0])

    def spread_column(use):
        await_halo(("row", use))
        line = added(AR.at[use, 0], ny)
        AS[use, 1] = line
        AR[use, 1, gx] = line
        send_all(("column", use), lambda p: AS.at[use, 1], AR.at[use, 1], gx, nx, in_column, a_s.at[use, 1], a_r.at[use, 1])

    def collected(use):
        await_halo(("column", use))
        line = added(AR.at[use, 1], nx)
        return jnp.sum(jnp.where(equal, line, 0.0), axis=1, keepdims=True)

    zeros = jnp.zeros((nc, LANES), F32)

    def sums_of(use, first, count, body, acc=None, begin=0, end=None):
        end = tiles if end is None else end

        def one(t, acc):
            i, b = t // (end - begin), begin + lax.rem(t, end - begin)
            at = pl.ds(pl.multiple_of(b * LANES, LANES), LANES)
            return tuple(a + v for a, v in zip(acc, body(i, at)))

        return lax.fori_loop(0, nr * (end - begin), one, (zeros,) * count if acc is None else acc)

    def store_sums(use, first, acc):
        for r, a in enumerate(acc):
            AW[use, first + r:first + r + 1] = jnp.sum(a, axis=0, keepdims=True)

    def scale_sums():
        def two(i, at):
            b0 = B[0, i + 1, :, at]
            weighted = D[i, :, at] * b0
            return weighted * b0, weighted * B[1, i + 1, :, at]

        AW[0] = zeros
        store_sums(0, 0, sums_of(0, 0, 2, two))
        spread_row(0)

    kept = {}

    def most_sums():
        pair = collected(0)
        rho = jnp.where(pair[0:1] > 0.0, pair[1:2] / pair[0:1], 1.0)
        kept["rho"] = rho

        def terms(fields, i, at):
            c0, c1, c2, c3 = fields
            m1 = c1 - c2
            m2 = c2 - 0.5 * (c3 + c1)
            v1 = c1 - rho * c0
            v2 = c2 - rho * (c0 - c1)
            v3 = c3 - rho * (c0 - 2.0 * (c1 + c2))
            weight = D[i, :, at]
            w0, w1, w2, w3 = (weight * v for v in (c0, v1, v2, v3))
            DV3[i, :, at] = w3
            n1 = m1 - rho * c1
            n2 = m2 - rho * c2
            n3 = rho * (c1 - 2.0 * (m1 + m2))
            return (
                w0 * c0, w1 * c0, w2 * c0, w3 * c0,
                w0 * c1, w1 * c1, w2 * c1, w3 * c1,
                w1 * n1, w2 * n1, w3 * n1,
                w2 * n2, w3 * n2,
                -(w3 * n3),
            )

        AW[1] = zeros
        acc = sums_of(1, 0, 14, lambda i, at: terms([B[k, i + 1, :, at] for k in range(4)], i, at), None, 0, tiles - 1)
        acc = sums_of(1, 0, 14, lambda i, at: terms([B[k, i + 1, :, at] + CE[k, nr + i, pad:pad + nc] for k in range(4)], i, at),
                      acc, tiles - 1, tiles)
        store_sums(1, 0, acc)

    def last_sum():
        def last(i, acc):
            value = DV3[i] * scaled_image(("b", 3), i)
            for b in range(tiles):
                acc = acc + value[:, b * LANES:(b + 1) * LANES]
            return acc

        def last_top(i, acc):
            return acc + DV3[i, :, top:nz] * scaled_image(("c", 3), i)

        await_halo(("b", 3))
        acc = lax.fori_loop(0, nr, last, zeros)
        await_halo(("c", 3))
        acc = lax.fori_loop(0, nr, last_top, acc)
        store_sums(1, 14, (acc,))
        spread_row(1)

    def answer():
        rho = kept["rho"]
        col = collected(1)
        e = [col[r:r + 1] for r in range(15)]
        g = e[0:4]
        H = {(0, 0): e[4], (1, 0): e[5], (2, 0): e[6], (3, 0): e[7], (1, 1): e[8], (2, 1): e[9], (3, 1): e[10],
             (2, 2): e[11], (3, 2): e[12], (3, 3): e[13] + e[14]}
        inv, low = {}, {}
        for j in range(4):
            pivot = H[j, j]
            for m in range(j):
                pivot = pivot - low[j, m] * H[j, m]
            inv[j] = jnp.where(pivot > 0.0, 1.0 / pivot, 0.0)
            for i in range(j + 1, 4):
                value = H[i, j]
                for m in range(j):
                    value = value - low[j, m] * H[i, m]
                H[i, j] = value
                low[i, j] = value * inv[j]
        y = list(g)
        for i in range(4):
            for m in range(i):
                y[i] = y[i] - low[i, m] * y[m]
        y = [y[i] * inv[i] for i in range(4)]
        for i in range(3, -1, -1):
            for m in range(i + 1, 4):
                y[i] = y[i] - low[m, i] * y[m]
        f0 = y[0] - rho * (y[1] + y[2] + y[3])
        f1 = y[1] + rho * (y[2] + 2.0 * y[3])
        f2 = y[2] + 2.0 * rho * y[3]

        y[0:3] = [f0, f1, f2]

        def extra(k, i):
            return CE[k, nr + i, pad:pad + nc]

        def finish(i):
            x_out[i] = X[i + 1] + ((y[0] * B[0, i + 1] + y[1] * B[1, i + 1]) + (y[2] * B[2, i + 1] + y[3] * B[3, i + 1]))
            x_out[i, :, top:nz] = x_out[i, :, top:nz] + (
                (y[0] * extra(0, i) + y[1] * extra(1, i)) + (y[2] * extra(2, i) + y[3] * extra(3, i)))

        rows(finish)

    def coefficients():
        loaded("flag", "dif", "vel")
        fluid_coefficients()

    def solid_start():
        loaded("cap", "q")
        await_halo(("k", 0))
        solid_coefficients()

    def send_input(name, key):
        loaded(key)
        stage_and_send(name)

    def fluid_step(k):
        await_halo(("u", k - 1))
        if k < SUBSTEPS:
            produce(("u", k), lambda i: fluid(("u", k - 1), i))
        else:
            rows(lambda i: u_out.__setitem__(i, fluid(("u", k - 1), i)))

    def low(k):
        await_halo(("l", k - 1))
        produce(("l", k), low_step(k - 1))

    def first_field():
        await_halo(("x", 0))
        produce(("b", 0), first_scaled)

    steps = {
        "T": collect_top, "L0": low_start, "LK": partners, "K": lambda: send_input(("k", 0), "k"), "X": lambda: send_input(("x", 0), "x"),
        "U0": lambda: send_input(("u", 0), "u"), "CF": coefficients, "G": ghosts, "L1": lambda: low(1), "L2": lambda: low(2),
        "L3": flux_home, "W": solid_start, "B0": first_field, "E": edge_copies, "EW": edge_coefficients, "C": flux_arrives, "R1": scale_sums, "R2": lambda: spread_column(0),
        "R3": most_sums, "H": last_sum, "A2": lambda: spread_column(1), "A3": answer,
    }
    for k in range(1, 4):
        steps[f"B{k}"] = functools.partial(field, k)
    for k in range(1, SUBSTEPS + 1):
        steps[f"U{k}"] = functools.partial(fluid_step, k)
    for name in ORDER:
        steps[name]()
    for left in leaving.values():
        left()


def solution(mesh):
    nx, ny = mesh.shape["gx"], mesh.shape["gy"]

    def local(u, dif, vel, flag, x, cap, k, q, look):
        nr, nc, nz = u.shape
        most = max(nx, ny)
        vm = lambda *shape: pltpu.VMEM(shape, F32)
        dma = lambda *shape: pltpu.SemaphoreType.DMA(shape)

        def linked(count, width):
            return [vm(count, nr + 2, nc, width), vm(count, 2, nr, width), vm(count, 2, nr, width)]

        def linked_one(width):
            return [vm(nr + 2, nc, width), vm(1, 2, nr, width), vm(1, 2, nr, width)]

        block = (nr, nc, nz)
        flags = pltpu.VMEM((nr, flag.shape[2], nc), jnp.int32)
        scratch = [
            *linked(4, nz), *linked(3, LANES), *linked_one(nz), *linked_one(nz), *linked(4, nz), *linked(1, LANES),
            vm(7, *block), vm(6, *block), vm(*block), vm(*block), vm(*block), vm(*block), vm(*block),
            vm(3, *block), vm(*block), flags, pltpu.VMEM(look.shape, jnp.int32),
            pltpu.VMEM((nr, nc, LANES), jnp.int32), vm(nr, nc, LANES), vm(nr, nc, LANES), vm(*block),
            vm(3, nc + 16, LANES), vm(3 * nr, nc + 16, LANES), vm(3 * nr, nc + 16, LANES), vm(8, 3 * nr, nc + 16, LANES), vm(4, 3 * nr, nc + 16, LANES),
            vm(nr, LANES), vm(ny, nr, LANES), vm(2, LANES), vm(3, ny, 2, LANES),
            vm(2, nc, LANES), vm(2, 2, 1, LANES), vm(2, 2, most, 1, LANES),
            dma(9), dma(EXCHANGES, 2), dma(EXCHANGES, 2), dma(EXCHANGES, 2), dma(EXCHANGES, 2),
            dma(), dma(), dma(8), dma(8), dma(3), dma(3), dma(2, 2), dma(2, 2),
        ]
        far = pl.BlockSpec(memory_space=pltpu.HBM)
        near = pl.BlockSpec(memory_space=pltpu.VMEM)
        flag = jnp.transpose(flag, (0, 2, 1))
        return pl.pallas_call(
            functools.partial(kernel, nx, ny),
            out_shape=(jax.ShapeDtypeStruct(block, F32), jax.ShapeDtypeStruct(block, F32)),
            in_specs=[far] * 9,
            out_specs=(near, near),
            scratch_shapes=scratch,
            compiler_params=pltpu.CompilerParams(collective_id=0, has_side_effects=True, vmem_limit_bytes=40 * 1024 * 1024),
            name="window",
        )(*(pltpu.with_memory_space_constraint(a, pltpu.HBM) for a in (u, dif, vel, flag, x, cap, k, q, look)))

    spec = P("gx", "gy", None)
    return jax.shard_map(
        local,
        mesh=mesh,
        in_specs=(spec, spec, P(None, "gx", "gy", None), spec, spec, spec, spec, spec, P("gx", "gy")),
        out_specs=(spec, spec),
        check_vma=False,
    )
```

time: 83.5 us -> 64.6 us (0.77)
  Pallas kernels: 73.4 us -> 62.2 us
  local copies, waits for them, and re-layouts: 9.04 us -> 1.41 us
    pallas_call x1, Pallas kernels: 73.4 us -> 62.2 us  [local(): pl.pallas_call(functools.partial(kernel, nx, ny), out_shape=(jax.ShapeDty...]
    unnamed x19 -> x2, local copies, waits for them, and re-layouts: 9.04 us -> 1.41 us
where the time goes in v2:
time: 64.6 us; the launch traced here: 64.2 us
  Pallas kernels  62.2 us (96%)
  local copies, waits for them, and re-layouts  1.41 us (2%)
    pallas_call x1, Pallas kernels, local(): pl.pallas_call(functools.partial(kernel, nx, ny), out_shape=(jax.ShapeDty...  62.2 us
    unnamed x2, local copies, waits for them, and re-layouts  1.41 us

profile of v2, /device:TPU:1, one launch (start us, length us, event | category | flops | bytes accessed | tf_op | source)
XLA Modules:
  0.0 64.2 jit_solution(14701556407489364181)
XLA Ops:
  0.6 62.2 %window.1 = (f32[4,16,1024]{2,1,0:T(8,128)S(1)}, f32[4,16,1024]{2,1,0:T(8,128)S(1)}) custom-call(f32[4,16,1024]{2,1,0:T(8,128)} %u_in.1, f32[4,16,1024]{2,1,0:T(8,128)} %dif_in.1, f32[3,4,16,1024]{3,2,1,0:T(8,128)} %vel_in.1, s32[4,8,16]{2,1,0:T(8,128)} %bitcast.1, f32[4,16,1024]{2,1,0:T(8,128)} %x_in.1, f32[4,16,1024]{2,1,0:T(8,128)} %cap_in.1, ...), custom_call_target="tpu_custom_call" | custom-call | tf_op jit(solution)/shard_map/window/pallas_call | solution.py:714
  62.8 0.7 %copy.13 = f32[4,16,1024]{2,1,0:T(8,128)} copy(f32[4,16,1024]{2,1,0:T(8,128)S(1)} %get-tuple-element.4) | data formatting | bytes 524288
  63.5 0.7 %copy.14 = f32[4,16,1024]{2,1,0:T(8,128)} copy(f32[4,16,1024]{2,1,0:T(8,128)S(1)} %get-tuple-element.5) | data formatting | bytes 524288

commit v3 on v2

--- a/solution.py
+++ b/solution.py
@@ -10,10 +10,10 @@
 MESH = pl.DeviceIdType.MESH
 SUBSTEPS = 4
 LANES = 128
-X_U, X_L, X_X, X_K, X_B, X_C, EXCHANGES = 0, 4, 7, 8, 9, 13, 14
+X_U, X_L, X_X, X_K, X_B, X_C, X_V, X_E, EXCHANGES = 0, 4, 7, 8, 9, 13, 14, 18, 19
 ORDER = (
-    "T", "L0", "K", "X", "LK", "CF", "G", "L1", "E", "W", "L2", "B0", "L3", "EW", "U0", "B1", "C", "R1", "B2", "U1",
-    "R2", "B3", "R3", "U2", "H", "U3", "A2", "U4", "A3",
+    "T", "L0", "K", "X", "LK", "CF", "G", "L1", "E", "W", "L2", "B0", "L3", "EW", "U0", "B1", "V0", "R1", "M", "B2", "C",
+    "R2", "B3", "U1", "V1", "R3", "H", "U2", "V2", "A2", "U3", "V3", "A3", "U4",
 )
 F32 = jnp.float32
 
@@ -21,7 +21,7 @@
 def kernel(nx, ny, u_in, dif_in, vel_in, flag_in, x_in, cap_in, k_in, q_in, look_in, u_out, x_out,
            U, HU, SU, L, HL, SL, X, HX, SX, K, HK, SK, B, HB, SB, C, HC, SC,
            CF, W, D, DI, CD, CAP, Q, VEL, DIF, FLAG, LOOK, LKC, GH, FX, DV3,
-           EP, EK, EC, WE, CE, TS, TR, PS, PR, AW, AS, AR,
+           EP, EK, EC, WE, CE, TS, TR, PS, PR, ES, ER, AW, AS, AR,
            in_sem, xs, xr, ys, yr, ts, tr, es, er, ps, pr, a_s, a_r):
     gx, gy = lax.axis_index("gx"), lax.axis_index("gy")
     nr, nc, nz = u_in.shape
@@ -31,6 +31,9 @@
     per = LANES // nc
     waiting, leaving = {}, {}
 
+    def turned(me, d, n):
+        return me + d - jnp.where(me + d >= n, n, 0)
+
     def spot(mx, my):
         return {"device_id": (mx, my), "device_id_type": MESH}
 
@@ -49,34 +52,34 @@
                 loads.pop(name).wait()
 
     EP[...] = jnp.zeros_like(EP)
+    ER[...] = jnp.zeros_like(ER)
     barrier = pltpu.get_barrier_semaphore()
 
     def greet_y(d, _):
-        pl.semaphore_signal(barrier, inc=1, **spot(gx, lax.rem(gy + d, ny)))
+        pl.semaphore_signal(barrier, inc=1, **spot(gx, turned(gy, d, ny)))
         return 0
 
     def greet_x(d, _):
-        pl.semaphore_signal(barrier, inc=1, **spot(lax.rem(gx + d, nx), gy))
+        pl.semaphore_signal(barrier, inc=1, **spot(turned(gx, d, nx), gy))
         return 0
-
-    def greet_beside(mx):
-        def one(d, _):
-            pl.semaphore_signal(barrier, inc=1, **spot(mx, lax.rem(gy + d, ny)))
-            return 0
-
-        lax.fori_loop(1, ny, one, 0)
 
     lax.fori_loop(1, ny, greet_y, 0)
     lax.fori_loop(1, nx, greet_x, 0)
-    beside = ((gx > 0, lax.rem(gx + nx - 1, nx)), (gx < nx - 1, lax.rem(gx + 1, nx)))
-    for there, mx in beside:
-        @pl.when(there)
-        def _(mx=mx):
-            greet_beside(mx)
+    corners = [(dx, dy) for dx in (-1, 1) for dy in (-1, 1)]
+
+    def in_grid(dx, dy):
+        return (gx + dx >= 0) & (gx + dx < nx) & (gy + dy >= 0) & (gy + dy < ny)
+
+    for dx, dy in corners:
+        @pl.when(in_grid(dx, dy))
+        def _(dx=dx, dy=dy):
+            pl.semaphore_signal(barrier, inc=1, **spot(lax.rem(gx + dx + nx, nx), lax.rem(gy + dy + ny, ny)))
 
     def all_here():
-        rows_beside = jnp.where(gx > 0, 1, 0) + jnp.where(gx < nx - 1, 1, 0)
-        pl.semaphore_wait(barrier, nx + ny - 2 + rows_beside * (ny - 1))
+        expected = nx + ny - 2
+        for dx, dy in corners:
+            expected = expected + jnp.where(in_grid(dx, dy), 1, 0)
+        pl.semaphore_wait(barrier, expected)
 
     for at_edge, row, side in ((gx == 0, 0, None), (gx == nx - 1, nr + 1, None), (gy == 0, None, 0), (gy == ny - 1, None, 1)):
         @pl.when(at_edge)
@@ -141,9 +144,21 @@
     links["x", 0] = (X, SX.at[0], HX.at[0], X_X)
     links["k", 0] = (K, SK.at[0], HK.at[0], X_K)
 
+    def x_copies(name, half=0):
+        ext, _, _, e = links[name]
+        if name[0] != "u":
+            return x_pair(ext, e)
+        lanes = pl.ds(half * (nz // 2), nz // 2)
+        return x_pair(ext.at[:, :, lanes], e + half * (X_V - X_U))
+
     def send_x(name):
-        ext, _, _, e = links[name]
-        start(x_pair(ext, e), gx, nx)
+        start(x_copies(name), gx, nx)
+
+    def send_rest(k):
+        pair = x_copies(("u", k), 1)
+        start(pair, gx, nx)
+        waiting["v", k] = lambda: arrive(pair, gx, nx)
+        leaving["v", k] = lambda: leave(pair, gx, nx)
 
     def send_y(name):
         ext, stage, rim, e = links[name]
@@ -151,11 +166,11 @@
 
         def came():
             arrive(y_pair(stage, rim, e), gy, ny)
-            arrive(x_pair(ext, e), gx, nx)
+            arrive(x_copies(name), gx, nx)
 
         def left():
             leave(y_pair(stage, rim, e), gy, ny)
-            leave(x_pair(ext, e), gx, nx)
+            leave(x_copies(name), gx, nx)
 
         waiting[name], leaving[name] = came, left
 
@@ -280,13 +295,13 @@
 
     def send_all(name, src_of, slots, me, n, peer_of, ssem, rsem):
         def one(d, _):
-            peer = lax.rem(me + d, n)
+            peer = turned(me, d, n)
             pltpu.make_async_remote_copy(src_of(peer), slots.at[me], ssem, rsem, **spot(*peer_of(peer))).start()
             return 0
 
         lax.fori_loop(1, n, one, 0)
         most = slots.at[pl.ds(0, n - 1)]
-        done = pltpu.make_async_remote_copy(most, most, ssem, rsem, **spot(*peer_of(lax.rem(me + 1, n))))
+        done = pltpu.make_async_remote_copy(most, most, ssem, rsem, **spot(*peer_of(turned(me, 1, n))))
         waiting[name], leaving[name] = done.wait_recv, done.wait_send
 
     sub = lax.broadcasted_iota(jnp.int32, (nc, LANES), 0)
@@ -354,34 +369,32 @@
         for i in range(nr):
             value = jnp.where(lane == i * nc + sub, FX[i][:, 0:1] / SUBSTEPS, value)
         PS[0:1] = jnp.sum(value, axis=0, keepdims=True)
-        PR[1, gy] = PS[...]
-        send_all("p", lambda p: PS, PR.at[1], gy, ny, in_row, ps.at[1], pr.at[1])
-        for there, mx, group in ((gx < nx - 1, lax.rem(gx + 1, nx), 0), (gx > 0, lax.rem(gx + nx - 1, nx), 2)):
-            @pl.when(there)
-            def _(mx=mx, group=group):
-                def one(d, _):
-                    peer = lax.rem(gy + d, ny)
-                    pltpu.make_async_remote_copy(PS, PR.at[group, gy], ps.at[group], pr.at[group], **spot(mx, peer)).start()
-                    return 0
-
-                lax.fori_loop(0, ny, one, 0)
-
-        def whole(group):
-            return pltpu.make_async_remote_copy(PR.at[group], PR.at[group], ps.at[group], pr.at[group], **spot(up_x, gy))
-
-        def came():
-            for there, group in ((gx > 0, 0), (gx < nx - 1, 2)):
-                @pl.when(there)
-                def _(group=group):
-                    whole(group).wait_recv()
-
-        def left():
-            for there, group in ((gx < nx - 1, 0), (gx > 0, 2)):
-                @pl.when(there)
-                def _(group=group):
-                    whole(group).wait_send()
-
-        waiting["p2"], leaving["p2"] = came, left
+        PR[gy] = PS[...]
+        send_all("p", lambda p: PS, PR, gy, ny, in_row, ps, pr)
+
+    def flux_beside():
+        await_halo("p")
+        column = (wide_sub + (gy * nc - pad)).astype(F32)
+        parts = []
+        for first in range(0, ny, 4):
+            total = jnp.zeros(wide, F32)
+            for s in range(first, min(first + 4, ny)):
+                total = jnp.where(PR[s, 1:2] == column, PR[s, 0:1], total)
+            parts.append(total)
+        total = functools.reduce(jnp.add, parts)
+        line = jnp.zeros(wide, F32)
+        for i in range(nr):
+            came = jnp.sum(jnp.where((wide_lane >= i * nc) & (wide_lane < (i + 1) * nc), total, 0.0), axis=1, keepdims=True)
+            line = jnp.where(wide_lane == i * wide[0] + wide_sub, came, line)
+            CE[0, nr + i] = jnp.where(wide_lane == LANES - 1, WE[7, nr + i] * came, 0.0)
+        ES[...] = jnp.sum(line, axis=0, keepdims=True)
+        pair = (
+            pltpu.make_async_remote_copy(ES, ER.at[0], xs.at[X_E, 0], xr.at[X_E, 0], **spot(up_x, gy)),
+            pltpu.make_async_remote_copy(ES, ER.at[1], xs.at[X_E, 1], xr.at[X_E, 1], **spot(dn_x, gy)),
+        )
+        start(pair, gx, nx)
+        waiting["m"] = lambda: arrive(pair, gx, nx)
+        leaving["m"] = lambda: leave(pair, gx, nx)
 
     def edge_copies():
         loaded("k", "cap")
@@ -444,25 +457,17 @@
         inverse = jnp.where(inside, 1.0 / jnp.where(inside, total, 1.0), 0.0)
         for n in range(6):
             WE[n, x:x + count] = faces[n] * inverse
+        for x_end in (0, 3 * nr - 1):
+            WE[7, x_end] = jnp.zeros(wide, F32)
         WE[6, x:x + count] = jnp.where(inside, cap, 0.0) * inverse
         WE[7, x:x + count] = inverse
 
     def flux_arrives():
-        await_halo("p", "p2")
-        column = (wide_sub + (gy * nc - pad)).astype(F32)
-        for group in range(3):
-            parts = []
-            for first in range(0, ny, 4):
-                total = jnp.zeros(wide, F32)
-                for s in range(first, min(first + 4, ny)):
-                    total = jnp.where(PR[group, s, 1:2] == column, PR[group, s, 0:1], total)
-                parts.append(total)
-            total = functools.reduce(jnp.add, parts)
-            there = {0: gx > 0, 1: gx >= 0, 2: gx < nx - 1}[group]
+        await_halo("m")
+        for side, group in ((0, 0), (1, 2)):
             for i in range(nr):
-                x = group * nr + i
-                came = jnp.sum(jnp.where((wide_lane >= i * nc) & (wide_lane < (i + 1) * nc), total, 0.0), axis=1, keepdims=True)
-                CE[0, x] = jnp.where((wide_lane == LANES - 1) & there, WE[7, x] * came, 0.0)
+                came = jnp.sum(jnp.where(wide_lane == i * wide[0] + wide_sub, ER[side], 0.0), axis=1, keepdims=True)
+                CE[0, group * nr + i] = jnp.where(wide_lane == LANES - 1, WE[7, group * nr + i] * came, 0.0)
         for k in range(1, 4):
             x, count = 1 + k, 3 * nr - 2 - 2 * k
             c, near = wide_around(CE.at[k - 1], x, count)
@@ -650,7 +655,7 @@
         stage_and_send(name)
 
     def fluid_step(k):
-        await_halo(("u", k - 1))
+        await_halo(("u", k - 1), ("v", k - 1))
         if k < SUBSTEPS:
             produce(("u", k), lambda i: fluid(("u", k - 1), i))
         else:
@@ -667,13 +672,14 @@
     steps = {
         "T": collect_top, "L0": low_start, "LK": partners, "K": lambda: send_input(("k", 0), "k"), "X": lambda: send_input(("x", 0), "x"),
         "U0": lambda: send_input(("u", 0), "u"), "CF": coefficients, "G": ghosts, "L1": lambda: low(1), "L2": lambda: low(2),
-        "L3": flux_home, "W": solid_start, "B0": first_field, "E": edge_copies, "EW": edge_coefficients, "C": flux_arrives, "R1": scale_sums, "R2": lambda: spread_column(0),
+        "L3": flux_home, "W": solid_start, "B0": first_field, "E": edge_copies, "EW": edge_coefficients, "M": flux_beside, "C": flux_arrives, "R1": scale_sums, "R2": lambda: spread_column(0),
         "R3": most_sums, "H": last_sum, "A2": lambda: spread_column(1), "A3": answer,
     }
     for k in range(1, 4):
         steps[f"B{k}"] = functools.partial(field, k)
     for k in range(1, SUBSTEPS + 1):
         steps[f"U{k}"] = functools.partial(fluid_step, k)
+        steps[f"V{k - 1}"] = functools.partial(send_rest, k - 1)
     for name in ORDER:
         steps[name]()
     for left in leaving.values():
@@ -703,10 +709,10 @@
             vm(3, *block), vm(*block), flags, pltpu.VMEM(look.shape, jnp.int32),
             pltpu.VMEM((nr, nc, LANES), jnp.int32), vm(nr, nc, LANES), vm(nr, nc, LANES), vm(*block),
             vm(3, nc + 16, LANES), vm(3 * nr, nc + 16, LANES), vm(3 * nr, nc + 16, LANES), vm(8, 3 * nr, nc + 16, LANES), vm(4, 3 * nr, nc + 16, LANES),
-            vm(nr, LANES), vm(ny, nr, LANES), vm(2, LANES), vm(3, ny, 2, LANES),
+            vm(nr, LANES), vm(ny, nr, LANES), vm(2, LANES), vm(ny, 2, LANES), vm(1, LANES), vm(2, 1, LANES),
             vm(2, nc, LANES), vm(2, 2, 1, LANES), vm(2, 2, most, 1, LANES),
             dma(9), dma(EXCHANGES, 2), dma(EXCHANGES, 2), dma(EXCHANGES, 2), dma(EXCHANGES, 2),
-            dma(), dma(), dma(8), dma(8), dma(3), dma(3), dma(2, 2), dma(2, 2),
+            dma(), dma(), dma(8), dma(8), dma(), dma(), dma(2, 2), dma(2, 2),
         ]
         far = pl.BlockSpec(memory_space=pltpu.HBM)
         near = pl.BlockSpec(memory_space=pltpu.VMEM)

time: 64.6 us -> 61.5 us (0.952)
  Pallas kernels: 62.2 us -> 59.2 us
    pallas_call x1, Pallas kernels: 62.2 us -> 59.2 us  [local(): pl.pallas_call(functools.partial(kernel, nx, ny), out_shape=(jax.ShapeDty...]
where the time goes in v3:
time: 61.5 us; the launch traced here: 61.2 us
  Pallas kernels  59.2 us (96%)
  local copies, waits for them, and re-layouts  1.41 us (2%)
  between operations  0.64 us (1%)
    pallas_call x1, Pallas kernels, local(): pl.pallas_call(functools.partial(kernel, nx, ny), out_shape=(jax.ShapeDty...  59.2 us
    unnamed x2, local copies, waits for them, and re-layouts  1.41 us

profile of v3, /device:TPU:1, one launch (start us, length us, event | category | flops | bytes accessed | tf_op | source)
XLA Modules:
  0.0 61.2 jit_solution(15976237536559702285)
XLA Ops:
  0.6 59.2 %window.1 = (f32[4,16,1024]{2,1,0:T(8,128)S(1)}, f32[4,16,1024]{2,1,0:T(8,128)S(1)}) custom-call(f32[4,16,1024]{2,1,0:T(8,128)} %u_in.1, f32[4,16,1024]{2,1,0:T(8,128)} %dif_in.1, f32[3,4,16,1024]{3,2,1,0:T(8,128)} %vel_in.1, s32[4,8,16]{2,1,0:T(8,128)} %bitcast.1, f32[4,16,1024]{2,1,0:T(8,128)} %x_in.1, f32[4,16,1024]{2,1,0:T(8,128)} %cap_in.1, ...), custom_call_target="tpu_custom_call" | custom-call | tf_op jit(solution)/shard_map/window/pallas_call | solution.py:720
  59.8 0.7 %copy.13 = f32[4,16,1024]{2,1,0:T(8,128)} copy(f32[4,16,1024]{2,1,0:T(8,128)S(1)} %get-tuple-element.4) | data formatting | bytes 524288
  60.5 0.7 %copy.14 = f32[4,16,1024]{2,1,0:T(8,128)} copy(f32[4,16,1024]{2,1,0:T(8,128)S(1)} %get-tuple-element.5) | data formatting | bytes 524288

commit v4 on v3

--- a/solution.py
+++ b/solution.py
@@ -65,6 +65,7 @@
 
     lax.fori_loop(1, ny, greet_y, 0)
     lax.fori_loop(1, nx, greet_x, 0)
+    greeted = [True]
     corners = [(dx, dy) for dx in (-1, 1) for dy in (-1, 1)]
 
     def in_grid(dx, dy):
@@ -76,6 +77,9 @@
             pl.semaphore_signal(barrier, inc=1, **spot(lax.rem(gx + dx + nx, nx), lax.rem(gy + dy + ny, ny)))
 
     def all_here():
+        if not greeted:
+            return
+        greeted.clear()
         expected = nx + ny - 2
         for dx, dy in corners:
             expected = expected + jnp.where(in_grid(dx, dy), 1, 0)
@@ -299,7 +303,7 @@
             pltpu.make_async_remote_copy(src_of(peer), slots.at[me], ssem, rsem, **spot(*peer_of(peer))).start()
             return 0
 
-        lax.fori_loop(1, n, one, 0)
+        lax.fori_loop(1, n, one, 0, unroll=True)
         most = slots.at[pl.ds(0, n - 1)]
         done = pltpu.make_async_remote_copy(most, most, ssem, rsem, **spot(*peer_of(turned(me, 1, n))))
         waiting[name], leaving[name] = done.wait_recv, done.wait_send
@@ -320,6 +324,7 @@
     def low_start():
         loaded("u")
         rows(lambda i: put(("l", 0), i, U[0, i + 1, :, 0:LANES]))
+        all_here()
         send_x(("l", 0))
         send_y(("l", 0))
 
@@ -591,8 +596,13 @@
         def last_top(i, acc):
             return acc + DV3[i, :, top:nz] * scaled_image(("c", 3), i)
 
-        await_halo(("b", 3))
-        acc = lax.fori_loop(0, nr, last, zeros)
+        name = ("b", 3)
+        _, stage, rim, e = links[name]
+        waiting.pop(name)
+        arrive(y_pair(stage, rim, e), gy, ny)
+        acc = lax.fori_loop(1, nr - 1, last, zeros)
+        arrive(x_copies(name), gx, nx)
+        acc = lax.fori_loop(0, 2, lambda t, total: last(t * (nr - 1), total), acc)
         await_halo(("c", 3))
         acc = lax.fori_loop(0, nr, last_top, acc)
         store_sums(1, 14, (acc,))
@@ -652,6 +662,7 @@
 
     def send_input(name, key):
         loaded(key)
+        all_here()
         stage_and_send(name)
 
     def fluid_step(k):

time: 61.5 us -> 61.1 us (level)
  no operation moved by 1% of the time
where the time goes in v4:
time: 61.1 us; the launch traced here: 61 us
  Pallas kernels  58.9 us (96%)
  local copies, waits for them, and re-layouts  1.41 us (2%)
  between operations  0.64 us (1%)
    pallas_call x1, Pallas kernels, local(): pl.pallas_call(functools.partial(kernel, nx, ny), out_shape=(jax.ShapeDty...  58.9 us
    unnamed x2, local copies, waits for them, and re-layouts  1.41 us

profile of v4, /device:TPU:1, one launch (start us, length us, event | category | flops | bytes accessed | tf_op | source)
XLA Modules:
  0.0 61.0 jit_solution(11590048666183838933)
XLA Ops:
  0.6 58.9 %window.1 = (f32[4,16,1024]{2,1,0:T(8,128)S(1)}, f32[4,16,1024]{2,1,0:T(8,128)S(1)}) custom-call(f32[4,16,1024]{2,1,0:T(8,128)} %u_in.1, f32[4,16,1024]{2,1,0:T(8,128)} %dif_in.1, f32[3,4,16,1024]{3,2,1,0:T(8,128)} %vel_in.1, s32[4,8,16]{2,1,0:T(8,128)} %bitcast.1, f32[4,16,1024]{2,1,0:T(8,128)} %x_in.1, f32[4,16,1024]{2,1,0:T(8,128)} %cap_in.1, ...), custom_call_target="tpu_custom_call" | custom-call | tf_op jit(solution)/shard_map/window/pallas_call | solution.py:731
  59.6 0.7 %copy.13 = f32[4,16,1024]{2,1,0:T(8,128)} copy(f32[4,16,1024]{2,1,0:T(8,128)S(1)} %get-tuple-element.4) | data formatting | bytes 524288
  60.3 0.7 %copy.14 = f32[4,16,1024]{2,1,0:T(8,128)} copy(f32[4,16,1024]{2,1,0:T(8,128)S(1)} %get-tuple-element.5) | data formatting | bytes 524288
